TPU v7x, 32 devices: a whole 2x2x4 slice. The times are simulated.
32 devices in a mesh: paper: 8 (over z, y), author: 4 (over x, core).
Axes of the slice: x: 2, y: 2, z: 4, core: 2. Of those that a mesh axis runs over, the one named last changes fastest.
Arguments:
- paper_feat: bfloat16 [2048, 1024], P('paper', 'author'), may hold values from -6 to 6
- author_feat: bfloat16 [2048, 1024], P('paper', 'author'), may hold values from -6 to 6
- cite_owner: int32 [384, 1], P('paper'), may hold values from 0 to 7; in each aligned block of 48 rows (0 to 47, 48 to 95, ...) at most 7 rows name the same one
- cite_source: int32 [384], P('paper'), may hold values from 0 to 1
- cite_target: int32 [384], P('paper'), may hold values from 0 to 1
- cite_edges: int32 [384], P('paper'), may hold values from 8 to 64
- cite_count: int32 [8], P('paper'), may hold values from 36 to 48, as said below
- citation_weight_tiles: bfloat16 [384, 128, 128], P('paper'), may hold values from 0 to 1
- write_owner: int32 [256, 1], P('paper'), may hold values from 0 to 7; in each aligned block of 32 rows (0 to 31, 32 to 63, ...) at most 5 rows name the same one
- write_paper: int32 [256], P('paper'), may hold values from 0 to 1
- write_author: int32 [256], P('paper'), may hold values from 0 to 1
- write_edges: int32 [256], P('paper'), may hold values from 8 to 64
- authorship_weight_tiles: bfloat16 [256, 128, 128], P('paper'), may hold values from 0 to 1
- w_self: bfloat16 [1024, 1024], replicated, may hold values from -0.1875 to 0.1875
- w_cite: bfloat16 [1024, 1024], replicated, may hold values from -0.1875 to 0.1875
- w_write: bfloat16 [1024, 1024], replicated, may hold values from -0.1875 to 0.1875
- cotangent: bfloat16 [2048, 1024], P('paper', 'author'), may hold values from -6 to 6
Outputs:
- paper_out: bfloat16 [2048, 1024], P('paper', 'author')
- paper_grad: bfloat16 [2048, 1024], P('paper', 'author')
- author_grad: bfloat16 [2048, 1024], P('paper', 'author')
Inputs may be any that keep to these rules, and one draw needn't show every extreme that they name: `cite_owner`: among the 48 tiles of one paper index (live or not), at most 7 have their source on any one paper index. The live tiles of a paper index are the first cite_count of its list; some paper index has all 48 live. `write_owner`: among the 32 tiles of one paper index, at most 5 take their author block from any one paper index.
All inputs are finite; a program needn't handle non-finite values.
Results may differ from a plain program's by a relative error of at most 0.007.
Values may be sent and summed in bfloat16 or wider, within the bound.
No kernel may reach another device: no remote copies, remote signals or barrier semaphores. Data moves between devices by JAX's collectives and lax.ppermute only.
A program may use at most 128 MiB of HBM per device.

v0:
```python
import functools
import jax
import jax.numpy as jnp
from jax import lax
from jax.experimental import pallas as pl
from jax.experimental.pallas import tpu as pltpu
from jax.sharding import PartitionSpec as P


def matmul(left, right):
    return jnp.dot(left, right, preferred_element_type=jnp.float32)


def matmul_flipped(left, right):
    return lax.dot_general(
        left, right, (((1,), (1,)), ((), ())), preferred_element_type=jnp.float32
    )


def matmul_rows(left, right):
    return lax.dot_general(
        left, right, (((0,), (0,)), ((), ())), preferred_element_type=jnp.float32
    )


def ring_order(count):
    if count % 2:
        return list(range(count))
    return list(range(0, count, 2)) + list(range(count - 1, 0, -2))


def ring_place(index, count):
    if count % 2:
        return index
    return jnp.where(index % 2 == 0, index // 2, count - (index + 1) // 2)


def ring_pairs(count, step):
    order = ring_order(count)
    return [(order[i], order[(i + step) % count]) for i in range(count)]


def ring_gather(block, count, first):
    ups = count // 2 if first > 0 else (count - 1) // 2
    blocks = {0: block}
    for reach, step in ((ups, 1), (count - 1 - ups, -1)):
        held = block
        for place in range(1, reach + 1):
            held = lax.ppermute(held, "paper", ring_pairs(count, step))
            blocks[-place * step % count] = held
    return [blocks[i] for i in range(count)]


def ring_scatter(partials, count, first):
    ups = count // 2 if first > 0 else (count - 1) // 2
    total = partials[0]
    for reach, step in ((ups, 1), (count - 1 - ups, -1)):
        if reach == 0:
            continue
        held = partials[reach * step % count]
        for place in range(reach - 1, 0, -1):
            held = lax.ppermute(held, "paper", ring_pairs(count, step))
            held = held.astype(jnp.float32) + partials[place * step % count].astype(jnp.float32)
            held = held.astype(jnp.bfloat16)
        held = lax.ppermute(held, "paper", ring_pairs(count, step))
        total = total + held.astype(jnp.float32)
    return total


def feature_gather(part, count):
    parts = {0: part}
    bit = count // 2
    while bit:
        pairs = [(i, i ^ bit) for i in range(count)]
        for r, held in list(parts.items()):
            parts[r ^ bit] = lax.ppermute(held, "author", pairs)
        bit //= 2
    return [parts[r] for r in range(count)]


VMEM_ELEMENTS = 1 << 20
VMEM_GRANT = 12 << 20
SMEM = pl.BlockSpec(memory_space=pltpu.SMEM)
VMEM = pl.BlockSpec(memory_space=pltpu.VMEM)


def adjacency_kernel(peers, counted, mine_ref, owner_ref, inner_ref, outer_ref, edges_ref, tiles_ref, *refs):
    out_ref, acc_ref = refs[-2:]
    groups, rows, cols = out_ref.shape
    side = tiles_ref.shape[1]
    across = cols // side
    down = rows // side
    here = ring_place(mine_ref[0], peers)
    limit = mine_ref[2] if counted else tiles_ref.shape[0]
    acc_ref[...] = jnp.zeros(acc_ref.shape, jnp.float32)

    def add(tile, carry):
        group = lax.rem(ring_place(owner_ref[tile], peers) - here + peers, peers)
        place = (group * down + inner_ref[tile]) * across + outer_ref[tile]
        edges = jnp.full((1, side), edges_ref[tile].astype(jnp.float32))
        live = jnp.where(tile < limit, 1.0, 0.0)
        acc_ref[place] += (live / edges) * tiles_ref[tile].astype(jnp.float32)
        return carry

    lax.fori_loop(0, tiles_ref.shape[0], add, 0, unroll=2)

    def store(group, carry):
        for i in range(down):
            for j in range(across):
                out_ref[group, i * side:(i + 1) * side, j * side:(j + 1) * side] = acc_ref[
                    (group * down + i) * across + j
                ].astype(jnp.bfloat16)
        return carry

    lax.fori_loop(0, groups, store, 0)


def adjacency(counted, mine, tables, tiles, peers, down, across, near, after):
    side = tiles.shape[1]
    call = pl.pallas_call(
        functools.partial(adjacency_kernel, peers, counted),
        out_shape=(pltpu.VMEM if near else jax.ShapeDtypeStruct)(
            (peers, down * side, across * side), jnp.bfloat16
        ),
        in_specs=[SMEM] * 5 + [VMEM] * (1 + len(after)),
        out_specs=VMEM,
        compiler_params=grant(near),
        scratch_shapes=[pltpu.VMEM((peers * down * across, side, side), jnp.float32)],
    )
    return call(
        mine, *tables, placed(tiles, near), *[placed(v, near) for v in after]
    )


def project_sum(mine, parts, weight_ref):
    quarter = parts[0].shape[1]
    total = None
    for r, part in enumerate(parts):
        start = pl.multiple_of((mine ^ r) * quarter, quarter)
        piece = matmul(part[...], weight_ref[pl.ds(start, quarter), :])
        total = piece if total is None else total + piece
    return total


def project_back_sum(mine, parts, weight_ref):
    quarter = parts[0].shape[1]
    own = pl.multiple_of(mine * quarter, quarter)
    total = None
    for r, part in enumerate(parts):
        start = pl.multiple_of((mine ^ r) * quarter, quarter)
        piece = matmul_flipped(part[...], weight_ref[pl.ds(own, quarter), pl.ds(start, quarter)])
        total = piece if total is None else total + piece
    return total


def fits(rows, cols):
    return rows * cols <= VMEM_ELEMENTS


def grant(near):
    return pltpu.CompilerParams(vmem_limit_bytes=VMEM_GRANT) if near else None


def placed(array, near):
    return pltpu.with_memory_space_constraint(array, pltpu.VMEM) if near else array


def run(kernel, mine, inputs, outs, near, after=(), kept=()):
    return pl.pallas_call(
        kernel,
        in_specs=[SMEM] + [VMEM] * (len(inputs) + len(after)),
        out_specs=[VMEM] * len(outs),
        out_shape=[
            (pltpu.VMEM if near and i not in kept else jax.ShapeDtypeStruct)(shape, dtype)
            for i, (shape, dtype) in enumerate(outs)
        ],
        compiler_params=grant(near),
    )(mine, *[placed(v, near) for v in inputs], *[placed(v, near) for v in after])


def fetch_kernel(weight_count, place_ref, count_ref, *refs):
    scalars_ref, sems = refs[-2:]
    refs = refs[:-2]
    sources, targets = refs[:len(refs) // 2], refs[len(refs) // 2:]
    quarter = targets[0].shape[1]
    own = pl.multiple_of(place_ref[1] * quarter, quarter)
    copies = []
    for i, (source, target) in enumerate(zip(sources, targets)):
        if i < weight_count:
            source = source.at[:, pl.ds(own, quarter)]
        copies.append(pltpu.make_async_copy(source, target, sems.at[i]))
    for copy in copies:
        copy.start()
    scalars_ref[0] = place_ref[0]
    scalars_ref[1] = place_ref[1]
    scalars_ref[2] = count_ref[0]
    for copy in copies:
        copy.wait()


def fetch(places, live, weights, tables, quarter, near):
    space = pltpu.VMEM if near else jax.ShapeDtypeStruct
    sources = [pltpu.with_memory_space_constraint(v, pltpu.HBM) for v in [*weights, *tables]]
    call = pl.pallas_call(
        functools.partial(fetch_kernel, len(weights)),
        in_specs=[SMEM, SMEM] + [pl.BlockSpec(memory_space=pltpu.HBM)] * len(sources),
        out_specs=[VMEM] * len(weights) + [SMEM] * (len(tables) + 1),
        out_shape=[space((weight.shape[0], quarter), weight.dtype) for weight in weights]
        + [pltpu.SMEM(table.shape, jnp.int32) for table in tables]
        + [pltpu.SMEM((3,), jnp.int32)],
        scratch_shapes=[pltpu.SemaphoreType.DMA((len(sources),))],
        compiler_params=grant(near),
    )
    *found, scalars = call(places, live, *sources)
    return found[:len(weights)], found[len(weights):], scalars


def enter_kernel(columns, mine_ref, *refs):
    parts, (cite_ref, self_ref) = refs[:columns], refs[columns:columns + 2]
    projected_ref, kept_ref = refs[-2:]
    mine = mine_ref[1]
    projected_ref[...] = project_sum(mine, parts, cite_ref).astype(jnp.bfloat16)
    kept_ref[...] = project_sum(mine, parts, self_ref)


def gather_kernel(peers, mine_ref, *refs):
    blocks, adj_ref, out_ref = refs[:peers], refs[peers], refs[-1]
    total = matmul(adj_ref[0], blocks[0][...])
    for i in range(1, peers):
        total = total + matmul(adj_ref[i], blocks[i][...])
    out_ref[...] = total.astype(jnp.bfloat16)


def more_kernel(columns, mine_ref, *refs):
    parts, (weight_ref, kept_ref, out_ref) = refs[:columns], refs[columns:]
    out_ref[...] = kept_ref[...] + project_sum(mine_ref[1], parts, weight_ref)


def layer_kernel(peers, mine_ref, *refs):
    blocks = refs[:peers]
    adj_ref, kept_ref, feat_ref, cot_ref, write_adj_ref, out_ref, grad_ref = refs[peers:peers + 7]
    partial_refs = refs[peers + 7:]
    preact = kept_ref[...]
    for i in range(peers):
        preact = preact + matmul(adj_ref[i], blocks[i][...])
    sigma = jax.nn.sigmoid(preact)
    out_ref[...] = (feat_ref[...].astype(jnp.float32) + preact * sigma).astype(jnp.bfloat16)
    slope = sigma * (1.0 + preact * (1.0 - sigma))
    grad = (cot_ref[...].astype(jnp.float32) * slope).astype(jnp.bfloat16)
    grad_ref[...] = grad
    for i in range(peers):
        partial_refs[i][...] = matmul_rows(write_adj_ref[i], grad).astype(partial_refs[i].dtype)


def back_kernel(columns, mine_ref, *refs):
    parts, (cite_ref, self_ref, adj_ref, cot_ref) = refs[:columns], refs[columns:columns + 4]
    partial_refs = refs[columns + 4:]
    mine = mine_ref[1]
    cite_grad = project_back_sum(mine, parts, cite_ref).astype(jnp.bfloat16)
    for i in range(len(partial_refs) - 1, 0, -1):
        partial_refs[i][...] = matmul_rows(adj_ref[i], cite_grad).astype(jnp.bfloat16)
    partial_refs[0][...] = (
        cot_ref[...].astype(jnp.float32)
        + project_back_sum(mine, parts, self_ref)
        + matmul_rows(adj_ref[0], cite_grad)
    )


def leave_kernel(columns, mine_ref, *refs):
    parts, (weight_ref, out_ref) = refs[:columns], refs[columns:]
    out_ref[...] = project_back_sum(mine_ref[1], parts, weight_ref).astype(jnp.bfloat16)


def body(
    paper_feat,
    author_feat,
    cite_owner,
    cite_source,
    cite_target,
    cite_edges,
    cite_count,
    citation_weight_tiles,
    write_owner,
    write_paper,
    write_author,
    write_edges,
    authorship_weight_tiles,
    w_self,
    w_cite,
    w_write,
    cotangent,
):
    peers = lax.axis_size("paper")
    columns = lax.axis_size("author")
    side = citation_weight_tiles.shape[1]
    paper_rows, quarter = paper_feat.shape
    author_rows = author_feat.shape[0]
    paper_blocks = paper_rows // side
    author_blocks = author_rows // side
    places = jnp.stack([lax.axis_index("paper"), lax.axis_index("author")])
    bf16 = jnp.bfloat16
    f32 = jnp.float32
    paper_tile = (paper_rows, quarter)
    author_tile = (author_rows, quarter)

    near = fits(peers * paper_rows, paper_rows)

    feats = feature_gather(paper_feat, columns)
    authors = ring_gather(author_feat, peers, 1)
    tables = [
        write_owner.reshape(-1), write_paper, write_author, write_edges,
        cite_owner.reshape(-1), cite_target, cite_source, cite_edges,
    ]
    windows, tables, mine = fetch(places, cite_count, [w_cite, w_self, w_write], tables, quarter, near)
    cite_window, self_window, write_window = windows
    projected, kept = run(
        functools.partial(enter_kernel, columns), mine, [*feats, cite_window, self_window],
        [(paper_tile, bf16), (paper_tile, f32)], near,
    )
    sources = ring_gather(projected, peers, -1)
    write_adj = adjacency(
        False, mine, tables[:4], authorship_weight_tiles, peers, paper_blocks, author_blocks,
        near, (projected,),
    )
    cite_adj = adjacency(
        True, mine, tables[4:], citation_weight_tiles, peers, paper_blocks, paper_blocks,
        near, (projected,),
    )
    write_sum, = run(
        functools.partial(gather_kernel, peers), mine, [*authors, write_adj],
        [(paper_tile, bf16)], near,
    )
    writes = feature_gather(write_sum, columns)
    kept, = run(
        functools.partial(more_kernel, columns), mine, [*writes, write_window, kept],
        [(paper_tile, f32)], near,
    )
    paper_out, grad_pre, *author_partials = run(
        functools.partial(layer_kernel, peers), mine,
        [*sources, cite_adj, kept, paper_feat, cotangent, write_adj],
        [(paper_tile, bf16), (paper_tile, bf16), (author_tile, f32)]
        + [(author_tile, bf16)] * (peers - 1), near, kept=(0,),
    )
    grads = feature_gather(grad_pre, columns)
    author_sum = ring_scatter(author_partials, peers, 1).astype(bf16)
    paper_partials = run(
        functools.partial(back_kernel, columns), mine,
        [*grads, w_cite, w_self, cite_adj, cotangent],
        [(paper_tile, f32)] + [(paper_tile, bf16)] * (peers - 1), near,
    )
    paper_grad = ring_scatter(paper_partials, peers, -1).astype(bf16)
    author_sums = feature_gather(author_sum, columns)
    author_grad, = run(
        functools.partial(leave_kernel, columns), mine, [*author_sums, w_write],
        [(author_tile, bf16)], near, kept=(0,),
    )
    return (paper_out, paper_grad, author_grad)


def solution(mesh):
    in_specs = (
        P("paper", "author"),
        P("paper", "author"),
        P("paper", None),
        P("paper"),
        P("paper"),
        P("paper"),
        P("paper"),
        P("paper", None, None),
        P("paper", None),
        P("paper"),
        P("paper"),
        P("paper"),
        P("paper", None, None),
        P(),
        P(),
        P(),
        P("paper", "author"),
    )
    out_specs = (P("paper", "author"), P("paper", "author"), P("paper", "author"))
    return jax.shard_map(body, mesh=mesh, in_specs=in_specs, out_specs=out_specs, check_vma=False)
```

profile of v0, /device:TPU:0, one launch (start us, length us, event | category | flops | bytes accessed | tf_op | source)
XLA Modules:
  0.0 78.1 jit_solution(15981314611057581978)
XLA Ops:
  0.6 3.1 %collective-permute-start.13 = (bf16[256,256]{1,0:T(8,128)(2,1)}, bf16[256,256]{1,0:T(8,128)(2,1)S(1)}, u32[]{:S(2)}, u32[]{:S(2)}) collective-permute-start(bf16[256,256]{1,0:T(8,128)(2,1)} %refs_0_.5), channel_id=1, source_target_pairs={{0,8},{8,16},{16,24},{24,28},{28,20},{20,12},{12,4},{4,0},{1,9},{9... | collective-permute-start | bytes 393224 | tf_op jit(solution)/shard_map/ppermute | solution.py:49
  3.7 1.5 %collective-permute-start.1 = (bf16[256,256]{1,0:T(8,128)(2,1)}, bf16[256,256]{1,0:T(8,128)(2,1)S(1)}, u32[]{:S(2)}, u32[]{:S(2)}) collective-permute-start(bf16[256,256]{1,0:T(8,128)(2,1)} %refs_10_.3), channel_id=1, source_target_pairs={{0,2},{1,3},{2,0},{3,1},{4,6},{5,7},{6,4},{7,5},{8,10},{9,11},{10,... | collective-permute-start | bytes 393224 | tf_op jit(solution)/shard_map/ppermute | solution.py:76
  5.7 1.7 %collective-permute-done.13.refs_7_ = bf16[256,256]{1,0:T(8,128)(2,1)S(1)} collective-permute-done((bf16[256,256]{1,0:T(8,128)(2,1)}, bf16[256,256]{1,0:T(8,128)(2,1)S(1)}, u32[]{:S(2)}, u32[]{:S(2)}) %collective-permute-start.13) | collective-permute-done | bytes 131104 | tf_op jit(solution)/shard_map/ppermute | solution.py:49
  7.4 1.8 %collective-permute-start.14 = (bf16[256,256]{1,0:T(8,128)(2,1)S(1)}, bf16[256,256]{1,0:T(8,128)(2,1)S(1)}, u32[]{:S(2)}, u32[]{:S(2)}) collective-permute-start(bf16[256,256]{1,0:T(8,128)(2,1)S(1)} %collective-permute-done.13.refs_7_), channel_id=1, source_target_pairs={{0,8},{8,16},{16,24},{24,28},{28,20},{20,12},{12,4},{4,0},{1,9},{9... | collective-permute-start | bytes 393224 | tf_op jit(solution)/shard_map/ppermute | solution.py:49
  10.4 2.1 %shard_map.184 = (bf16[1024,256]{1,0:T(8,128)(2,1)S(1)}, bf16[1024,256]{1,0:T(8,128)(2,1)S(1)}, bf16[1024,256]{1,0:T(8,128)(2,1)S(1)}, s32[32]{0:T(128)S(4)}, s3...) custom-call(s32[2]{0:T(128)S(1)} %pad_add_fusion.place_ref, ...), custom_call_target="tpu_custom_call" | custom-call | tf_op jit(solution)/shard_map/pallas_call | solution.py:214
  12.8 1.8 %collective-permute-start.15 = (bf16[256,256]{1,0:T(8,128)(2,1)S(1)}, bf16[256,256]{1,0:T(8,128)(2,1)S(1)}, u32[]{:S(2)}, u32[]{:S(2)}) collective-permute-start(bf16[256,256]{1,0:T(8,128)(2,1)S(1)} %collective-permute-done.14.refs_6_), channel_id=1, source_target_pairs={{0,8},{8,16},{16,24},{24,28},{28,20},{20,12},{12,4},{4,0},{1,9},{9... | collective-permute-start | bytes 393224 | tf_op jit(solution)/shard_map/ppermute | solution.py:49
  15.4 3.5 %collective-permute-done.11.refs_2_ = bf16[256,256]{1,0:T(8,128)(2,1)S(1)} collective-permute-done((bf16[256,256]{1,0:T(8,128)(2,1)S(1)}, bf16[256,256]{1,0:T(8,128)(2,1)S(1)}, u32[]{:S(2)}, u32[]{:S(2)}) %collective-permute-start.11) | collective-permute-done | bytes 131104 | tf_op jit(solution)/shard_map/ppermute | solution.py:49
  19.1 1.8 %collective-permute-start.16 = (bf16[256,256]{1,0:T(8,128)(2,1)S(1)}, bf16[256,256]{1,0:T(8,128)(2,1)S(1)}, u32[]{:S(2)}, u32[]{:S(2)}) collective-permute-start(bf16[256,256]{1,0:T(8,128)(2,1)S(1)} %collective-permute-done.15.refs_5_), channel_id=1, source_target_pairs={{0,8},{8,16},{16,24},{24,28},{28,20},{20,12},{12,4},{4,0},{1,9},{9... | collective-permute-start | bytes 393224 | tf_op jit(solution)/shard_map/ppermute | solution.py:49
  20.9 1.6 %collective-permute-start.7 = (bf16[256,256]{1,0:T(8,128)(2,1)S(1)}, bf16[256,256]{1,0:T(8,128)(2,1)S(1)}, u32[]{:S(2)}, u32[]{:S(2)}) collective-permute-start(bf16[256,256]{1,0:T(8,128)(2,1)S(1)} %get-tuple-element.38.refs_0_), channel_id=1, source_target_pairs={{0,8},{8,16},{16,24},{24,28},{28,20},{20,12},{12,4},{4,0},{1,9},{9... | collective-permute-start | bytes 393224 | tf_op jit(solution)/shard_map/ppermute | solution.py:49
  25.3 1.6 %collective-permute-start.18 = (bf16[256,256]{1,0:T(8,128)(2,1)S(1)}, bf16[256,256]{1,0:T(8,128)(2,1)S(1)}, u32[]{:S(2)}, u32[]{:S(2)}) collective-permute-start(bf16[256,256]{1,0:T(8,128)(2,1)S(1)} %shard_map.188.refs_0_), channel_id=1, source_target_pairs={{0,2},{1,3},{2,0},{3,1},{4,6},{5,7},{6,4},{7,5},{8,10},{9,11},{10,... | collective-permute-start | bytes 393224 | tf_op jit(solution)/shard_map/ppermute | solution.py:76
  26.9 1.6 %collective-permute-start.8 = (bf16[256,256]{1,0:T(8,128)(2,1)S(1)}, bf16[256,256]{1,0:T(8,128)(2,1)S(1)}, u32[]{:S(2)}, u32[]{:S(2)}) collective-permute-start(bf16[256,256]{1,0:T(8,128)(2,1)S(1)} %collective-permute-done.7.refs_7_), channel_id=1, source_target_pairs={{0,8},{8,16},{16,24},{24,28},{28,20},{20,12},{12,4},{4,0},{1,9},{9... | collective-permute-start | bytes 393224 | tf_op jit(solution)/shard_map/ppermute | solution.py:49
  28.9 1.4 %collective-permute-done.18.refs_2_ = bf16[256,256]{1,0:T(8,128)(2,1)S(1)} collective-permute-done((bf16[256,256]{1,0:T(8,128)(2,1)S(1)}, bf16[256,256]{1,0:T(8,128)(2,1)S(1)}, u32[]{:S(2)}, u32[]{:S(2)}) %collective-permute-start.18) | collective-permute-done | bytes 131104 | tf_op jit(solution)/shard_map/ppermute | solution.py:76
  30.4 1.5 %collective-permute-done.8.refs_6_ = bf16[256,256]{1,0:T(8,128)(2,1)S(1)} collective-permute-done((bf16[256,256]{1,0:T(8,128)(2,1)S(1)}, bf16[256,256]{1,0:T(8,128)(2,1)S(1)}, u32[]{:S(2)}, u32[]{:S(2)}) %collective-permute-start.8) | collective-permute-done | bytes 131104 | tf_op jit(solution)/shard_map/ppermute | solution.py:49
  31.9 1.6 %collective-permute-start.9 = (bf16[256,256]{1,0:T(8,128)(2,1)S(1)}, bf16[256,256]{1,0:T(8,128)(2,1)S(1)}, u32[]{:S(2)}, u32[]{:S(2)}) collective-permute-start(bf16[256,256]{1,0:T(8,128)(2,1)S(1)} %collective-permute-done.8.refs_6_), channel_id=1, source_target_pairs={{0,8},{8,16},{16,24},{24,28},{28,20},{20,12},{12,4},{4,0},{1,9},{9... | collective-permute-start | bytes 393224 | tf_op jit(solution)/shard_map/ppermute | solution.py:49
  33.9 1.4 %shard_map.186.refs_8_.refs_6_ = bf16[8,256,256]{2,1,0:T(8,128)(2,1)S(1)} custom-call(s32[3]{0:T(128)S(4)} %get-tuple-element.35.mine_ref, s32[48]{0:T(128)S(4)} %get-tuple-element.39.owner_ref, s32[48]{0:T(128)S(4)} %get-tuple-element.40.inner_ref, s32[48]{0:T(128)S(4)} %get-tuple-element.41.outer_ref, s32[48]{0:T(128)S(4)} %get-tuple-element.42.edges_ref, ...), custom_call_target="tpu_custom_call" | custom-call | tf_op jit(solution)/shard_map/pallas_call | solution.py:130
  36.8 1.6 %collective-permute-done.6.refs_4_ = bf16[256,256]{1,0:T(8,128)(2,1)S(1)} collective-permute-done((bf16[256,256]{1,0:T(8,128)(2,1)S(1)}, bf16[256,256]{1,0:T(8,128)(2,1)S(1)}, u32[]{:S(2)}, u32[]{:S(2)}) %collective-permute-start.6) | collective-permute-done | bytes 131104 | tf_op jit(solution)/shard_map/ppermute | solution.py:49
  38.4 1.4 %shard_map.190 = (bf16[256,256]{1,0:T(8,128)(2,1)}, bf16[256,256]{1,0:T(8,128)(2,1)S(1)}, f32[256,256]{1,0:T(8,128)S(1)}, bf16[256,256]{1,0:T(8,128)(2,1)S(1)}, ...) custom-call(s32[3]{0:T(128)S(4)} %get-tuple-element.35.mine_ref, ...), custom_call_target="tpu_custom_call" | custom-call | tf_op jit(solution)/shard_map/pallas_call | solution.py:169
  39.8 1.6 %collective-permute-start.30 = (bf16[256,256]{1,0:T(8,128)(2,1)S(1)}, bf16[256,256]{1,0:T(8,128)(2,1)S(1)}, u32[]{:S(2)}, u32[]{:S(2)}) collective-permute-start(bf16[256,256]{1,0:T(8,128)(2,1)S(1)} %get-tuple-element.60), channel_id=1, source_target_pairs={{0,8},{8,16},{16,24},{24,28},{28,20},{20,12},{12,4},{4,0},{1,9},{9... | collective-permute-start | bytes 393224 | tf_op jit(solution)/shard_map/ppermute | solution.py:62
  42.7 2.1 %collective-permute-done.30 = bf16[256,256]{1,0:T(8,128)(2,1)S(1)} collective-permute-done((bf16[256,256]{1,0:T(8,128)(2,1)S(1)}, bf16[256,256]{1,0:T(8,128)(2,1)S(1)}, u32[]{:S(2)}, u32[]{:S(2)}) %collective-permute-start.30) | collective-permute-done | bytes 131104 | tf_op jit(solution)/shard_map/ppermute | solution.py:62
  44.9 1.6 %collective-permute-start.31 = (bf16[256,256]{1,0:T(8,128)(2,1)S(1)}, bf16[256,256]{1,0:T(8,128)(2,1)S(1)}, u32[]{:S(2)}, u32[]{:S(2)}) collective-permute-start(bf16[256,256]{1,0:T(8,128)(2,1)S(1)} %add_convert_fusion.5), channel_id=1, source_target_pairs={{0,8},{8,16},{16,24},{24,28},{28,20},{20,12},{12,4},{4,0},{1,9},{9... | collective-permute-start | bytes 393224 | tf_op jit(solution)/shard_map/ppermute | solution.py:62
  46.5 1.7 %collective-permute-done.34 = bf16[256,256]{1,0:T(8,128)(2,1)S(1)} collective-permute-done((bf16[256,256]{1,0:T(8,128)(2,1)S(1)}, bf16[256,256]{1,0:T(8,128)(2,1)S(1)}, u32[]{:S(2)}, u32[]{:S(2)}) %collective-permute-start.34) | collective-permute-done | bytes 131104 | tf_op jit(solution)/shard_map/ppermute | solution.py:62
  50.0 1.6 %collective-permute-start.32 = (bf16[256,256]{1,0:T(8,128)(2,1)S(1)}, bf16[256,256]{1,0:T(8,128)(2,1)S(1)}, u32[]{:S(2)}, u32[]{:S(2)}) collective-permute-start(bf16[256,256]{1,0:T(8,128)(2,1)S(1)} %add_convert_fusion.4), channel_id=1, source_target_pairs={{0,8},{8,16},{16,24},{24,28},{28,20},{20,12},{12,4},{4,0},{1,9},{9... | collective-permute-start | bytes 393224 | tf_op jit(solution)/shard_map/ppermute | solution.py:62
  51.6 1.7 %collective-permute-done.35 = bf16[256,256]{1,0:T(8,128)(2,1)S(1)} collective-permute-done((bf16[256,256]{1,0:T(8,128)(2,1)S(1)}, bf16[256,256]{1,0:T(8,128)(2,1)S(1)}, u32[]{:S(2)}, u32[]{:S(2)}) %collective-permute-start.35) | collective-permute-done | bytes 131104 | tf_op jit(solution)/shard_map/ppermute | solution.py:62
  54.8 1.6 %collective-permute-start.23 = (bf16[256,256]{1,0:T(8,128)(2,1)S(1)}, bf16[256,256]{1,0:T(8,128)(2,1)S(1)}, u32[]{:S(2)}, u32[]{:S(2)}) collective-permute-start(bf16[256,256]{1,0:T(8,128)(2,1)S(1)} %get-tuple-element.52), channel_id=1, source_target_pairs={{0,8},{8,16},{16,24},{24,28},{28,20},{20,12},{12,4},{4,0},{1,9},{9... | collective-permute-start | bytes 393224 | tf_op jit(solution)/shard_map/ppermute | solution.py:62
  57.0 1.6 %collective-permute-start.33 = (bf16[256,256]{1,0:T(8,128)(2,1)S(1)}, bf16[256,256]{1,0:T(8,128)(2,1)S(1)}, u32[]{:S(2)}, u32[]{:S(2)}) collective-permute-start(bf16[256,256]{1,0:T(8,128)(2,1)S(1)} %add_convert_fusion.3), channel_id=1, source_target_pairs={{0,8},{8,16},{16,24},{24,28},{28,20},{20,12},{12,4},{4,0},{1,9},{9... | collective-permute-start | bytes 393224 | tf_op jit(solution)/shard_map/ppermute | solution.py:65
  58.6 1.9 %collective-permute-done.23 = bf16[256,256]{1,0:T(8,128)(2,1)S(1)} collective-permute-done((bf16[256,256]{1,0:T(8,128)(2,1)S(1)}, bf16[256,256]{1,0:T(8,128)(2,1)S(1)}, u32[]{:S(2)}, u32[]{:S(2)}) %collective-permute-start.23) | collective-permute-done | bytes 131104 | tf_op jit(solution)/shard_map/ppermute | solution.py:62
  60.6 1.6 %collective-permute-start.24 = (bf16[256,256]{1,0:T(8,128)(2,1)S(1)}, bf16[256,256]{1,0:T(8,128)(2,1)S(1)}, u32[]{:S(2)}, u32[]{:S(2)}) collective-permute-start(bf16[256,256]{1,0:T(8,128)(2,1)S(1)} %add_convert_fusion.11), channel_id=1, source_target_pairs={{0,8},{8,16},{16,24},{24,28},{28,20},{20,12},{12,4},{4,0},{1,9},{9... | collective-permute-start | bytes 393224 | tf_op jit(solution)/shard_map/ppermute | solution.py:62
  63.2 1.3 %collective-permute-start.38 = (bf16[256,256]{1,0:T(8,128)(2,1)S(1)}, bf16[256,256]{1,0:T(8,128)(2,1)S(1)}, u32[]{:S(2)}, u32[]{:S(2)}) collective-permute-start(bf16[256,256]{1,0:T(8,128)(2,1)S(1)} %add_convert_fusion.refs_0_), channel_id=1, source_target_pairs={{0,2},{1,3},{2,0},{3,1},{4,6},{5,7},{6,4},{7,5},{8,10},{9,11},{10,... | collective-permute-start | bytes 393224 | tf_op jit(solution)/shard_map/ppermute | solution.py:76
  64.5 2.8 %collective-permute-done.27 = bf16[256,256]{1,0:T(8,128)(2,1)S(1)} collective-permute-done((bf16[256,256]{1,0:T(8,128)(2,1)S(1)}, bf16[256,256]{1,0:T(8,128)(2,1)S(1)}, u32[]{:S(2)}, u32[]{:S(2)}) %collective-permute-start.27) | collective-permute-done | bytes 131104 | tf_op jit(solution)/shard_map/ppermute | solution.py:62
  67.8 1.6 %collective-permute-start.25 = (bf16[256,256]{1,0:T(8,128)(2,1)S(1)}, bf16[256,256]{1,0:T(8,128)(2,1)S(1)}, u32[]{:S(2)}, u32[]{:S(2)}) collective-permute-start(bf16[256,256]{1,0:T(8,128)(2,1)S(1)} %add_convert_fusion.10), channel_id=1, source_target_pairs={{0,8},{8,16},{16,24},{24,28},{28,20},{20,12},{12,4},{4,0},{1,9},{9... | collective-permute-start | bytes 393224 | tf_op jit(solution)/shard_map/ppermute | solution.py:65
  69.5 2.8 %collective-permute-done.28 = bf16[256,256]{1,0:T(8,128)(2,1)S(1)} collective-permute-done((bf16[256,256]{1,0:T(8,128)(2,1)S(1)}, bf16[256,256]{1,0:T(8,128)(2,1)S(1)}, u32[]{:S(2)}, u32[]{:S(2)}) %collective-permute-start.28) | collective-permute-done | bytes 131104 | tf_op jit(solution)/shard_map/ppermute | solution.py:62
  73.9 3.5 %collective-permute-done.29 = bf16[256,256]{1,0:T(8,128)(2,1)S(1)} collective-permute-done((bf16[256,256]{1,0:T(8,128)(2,1)S(1)}, bf16[256,256]{1,0:T(8,128)(2,1)S(1)}, u32[]{:S(2)}, u32[]{:S(2)}) %collective-permute-start.29) | collective-permute-done | bytes 131104 | tf_op jit(solution)/shard_map/ppermute | solution.py:65
  (86 shorter events, 16.5 us)
Async XLA Ops:
  0.6 6.8 %collective-permute-start.13 = (bf16[256,256]{1,0:T(8,128)(2,1)}, bf16[256,256]{1,0:T(8,128)(2,1)S(1)}, u32[]{:S(2)}, u32[]{:S(2)}) collective-permute-start(bf16[256,256]{1,0:T(8,128)(2,1)} %refs_0_.5), channel_id=1, source_target_pairs={{0,8},{8,16},{16,24},{24,28},{28,20},{20,12},{12,4},{4,0},{1,9},{9... | collective-permute-start | bytes 393224 | tf_op jit(solution)/shard_map/ppermute | solution.py:49
  3.7 5.5 %collective-permute-start.1 = (bf16[256,256]{1,0:T(8,128)(2,1)}, bf16[256,256]{1,0:T(8,128)(2,1)S(1)}, u32[]{:S(2)}, u32[]{:S(2)}) collective-permute-start(bf16[256,256]{1,0:T(8,128)(2,1)} %refs_10_.3), channel_id=1, source_target_pairs={{0,2},{1,3},{2,0},{3,1},{4,6},{5,7},{6,4},{7,5},{8,10},{9,11},{10,... | collective-permute-start | bytes 393224 | tf_op jit(solution)/shard_map/ppermute | solution.py:76
  5.2 7.3 %collective-permute-start.10 = (bf16[256,256]{1,0:T(8,128)(2,1)}, bf16[256,256]{1,0:T(8,128)(2,1)S(1)}, u32[]{:S(2)}, u32[]{:S(2)}) collective-permute-start(bf16[256,256]{1,0:T(8,128)(2,1)} %refs_0_.5), channel_id=1, source_target_pairs={{0,4},{8,0},{16,8},{24,16},{28,24},{20,28},{12,20},{4,12},{1,5},{9... | collective-permute-start | bytes 393224 | tf_op jit(solution)/shard_map/ppermute | solution.py:49
  7.4 5.5 %collective-permute-start.14 = (bf16[256,256]{1,0:T(8,128)(2,1)S(1)}, bf16[256,256]{1,0:T(8,128)(2,1)S(1)}, u32[]{:S(2)}, u32[]{:S(2)}) collective-permute-start(bf16[256,256]{1,0:T(8,128)(2,1)S(1)} %collective-permute-done.13.refs_7_), channel_id=1, source_target_pairs={{0,8},{8,16},{16,24},{24,28},{28,20},{20,12},{12,4},{4,0},{1,9},{9... | collective-permute-start | bytes 393224 | tf_op jit(solution)/shard_map/ppermute | solution.py:49
  9.2 5.5 %collective-permute-start = (bf16[256,256]{1,0:T(8,128)(2,1)}, bf16[256,256]{1,0:T(8,128)(2,1)S(1)}, u32[]{:S(2)}, u32[]{:S(2)}) collective-permute-start(bf16[256,256]{1,0:T(8,128)(2,1)} %refs_10_.3), channel_id=1, source_target_pairs={{0,1},{1,0},{2,3},{3,2},{4,5},{5,4},{6,7},{7,6},{8,9},{9,8},{10,11... | collective-permute-start | bytes 393224 | tf_op jit(solution)/shard_map/ppermute | solution.py:76
  9.2 5.5 %collective-permute-start.2 = (bf16[256,256]{1,0:T(8,128)(2,1)S(1)}, bf16[256,256]{1,0:T(8,128)(2,1)S(1)}, u32[]{:S(2)}, u32[]{:S(2)}) collective-permute-start(bf16[256,256]{1,0:T(8,128)(2,1)S(1)} %collective-permute-done.1.refs_2_), channel_id=1, source_target_pairs={{0,1},{1,0},{2,3},{3,2},{4,5},{5,4},{6,7},{7,6},{8,9},{9,8},{10,11... | collective-permute-start | bytes 393224 | tf_op jit(solution)/shard_map/ppermute | solution.py:76
  12.6 6.3 %collective-permute-start.11 = (bf16[256,256]{1,0:T(8,128)(2,1)S(1)}, bf16[256,256]{1,0:T(8,128)(2,1)S(1)}, u32[]{:S(2)}, u32[]{:S(2)}) collective-permute-start(bf16[256,256]{1,0:T(8,128)(2,1)S(1)} %collective-permute-done.10.refs_1_), channel_id=1, source_target_pairs={{0,4},{8,0},{16,8},{24,16},{28,24},{20,28},{12,20},{4,12},{1,5},{9... | collective-permute-start | bytes 393224 | tf_op jit(solution)/shard_map/ppermute | solution.py:49
  12.8 6.2 %collective-permute-start.15 = (bf16[256,256]{1,0:T(8,128)(2,1)S(1)}, bf16[256,256]{1,0:T(8,128)(2,1)S(1)}, u32[]{:S(2)}, u32[]{:S(2)}) collective-permute-start(bf16[256,256]{1,0:T(8,128)(2,1)S(1)} %collective-permute-done.14.refs_6_), channel_id=1, source_target_pairs={{0,8},{8,16},{16,24},{24,28},{28,20},{20,12},{12,4},{4,0},{1,9},{9... | collective-permute-start | bytes 393224 | tf_op jit(solution)/shard_map/ppermute | solution.py:49
  15.1 7.3 %collective-permute-start.3 = (bf16[256,256]{1,0:T(8,128)(2,1)S(1)}, bf16[256,256]{1,0:T(8,128)(2,1)S(1)}, u32[]{:S(2)}, u32[]{:S(2)}) collective-permute-start(bf16[256,256]{1,0:T(8,128)(2,1)S(1)} %get-tuple-element.38.refs_0_), channel_id=1, source_target_pairs={{0,4},{8,0},{16,8},{24,16},{28,24},{20,28},{12,20},{4,12},{1,5},{9... | collective-permute-start | bytes 393224 | tf_op jit(solution)/shard_map/ppermute | solution.py:49
  18.8 6.1 %collective-permute-start.12 = (bf16[256,256]{1,0:T(8,128)(2,1)S(1)}, bf16[256,256]{1,0:T(8,128)(2,1)S(1)}, u32[]{:S(2)}, u32[]{:S(2)}) collective-permute-start(bf16[256,256]{1,0:T(8,128)(2,1)S(1)} %collective-permute-done.11.refs_2_), channel_id=1, source_target_pairs={{0,4},{8,0},{16,8},{24,16},{28,24},{20,28},{12,20},{4,12},{1,5},{9... | collective-permute-start | bytes 393224 | tf_op jit(solution)/shard_map/ppermute | solution.py:49
  19.1 5.8 %collective-permute-start.16 = (bf16[256,256]{1,0:T(8,128)(2,1)S(1)}, bf16[256,256]{1,0:T(8,128)(2,1)S(1)}, u32[]{:S(2)}, u32[]{:S(2)}) collective-permute-start(bf16[256,256]{1,0:T(8,128)(2,1)S(1)} %collective-permute-done.15.refs_5_), channel_id=1, source_target_pairs={{0,8},{8,16},{16,24},{24,28},{28,20},{20,12},{12,4},{4,0},{1,9},{9... | collective-permute-start | bytes 393224 | tf_op jit(solution)/shard_map/ppermute | solution.py:49
  20.9 6.0 %collective-permute-start.7 = (bf16[256,256]{1,0:T(8,128)(2,1)S(1)}, bf16[256,256]{1,0:T(8,128)(2,1)S(1)}, u32[]{:S(2)}, u32[]{:S(2)}) collective-permute-start(bf16[256,256]{1,0:T(8,128)(2,1)S(1)} %get-tuple-element.38.refs_0_), channel_id=1, source_target_pairs={{0,8},{8,16},{16,24},{24,28},{28,20},{20,12},{12,4},{4,0},{1,9},{9... | collective-permute-start | bytes 393224 | tf_op jit(solution)/shard_map/ppermute | solution.py:49
  22.4 6.0 %collective-permute-start.4 = (bf16[256,256]{1,0:T(8,128)(2,1)S(1)}, bf16[256,256]{1,0:T(8,128)(2,1)S(1)}, u32[]{:S(2)}, u32[]{:S(2)}) collective-permute-start(bf16[256,256]{1,0:T(8,128)(2,1)S(1)} %collective-permute-done.3.refs_1_), channel_id=1, source_target_pairs={{0,4},{8,0},{16,8},{24,16},{28,24},{20,28},{12,20},{4,12},{1,5},{9... | collective-permute-start | bytes 393224 | tf_op jit(solution)/shard_map/ppermute | solution.py:49
  25.3 5.0 %collective-permute-start.18 = (bf16[256,256]{1,0:T(8,128)(2,1)S(1)}, bf16[256,256]{1,0:T(8,128)(2,1)S(1)}, u32[]{:S(2)}, u32[]{:S(2)}) collective-permute-start(bf16[256,256]{1,0:T(8,128)(2,1)S(1)} %shard_map.188.refs_0_), channel_id=1, source_target_pairs={{0,2},{1,3},{2,0},{3,1},{4,6},{5,7},{6,4},{7,5},{8,10},{9,11},{10,... | collective-permute-start | bytes 393224 | tf_op jit(solution)/shard_map/ppermute | solution.py:76
  28.9 6.4 %collective-permute-start.17 = (bf16[256,256]{1,0:T(8,128)(2,1)S(1)}, bf16[256,256]{1,0:T(8,128)(2,1)S(1)}, u32[]{:S(2)}, u32[]{:S(2)}) collective-permute-start(bf16[256,256]{1,0:T(8,128)(2,1)S(1)} %shard_map.188.refs_0_), channel_id=1, source_target_pairs={{0,1},{1,0},{2,3},{3,2},{4,5},{5,4},{6,7},{7,6},{8,9},{9,8},{10,11... | collective-permute-start | bytes 393224 | tf_op jit(solution)/shard_map/ppermute | solution.py:76
  39.8 5.0 %collective-permute-start.30 = (bf16[256,256]{1,0:T(8,128)(2,1)S(1)}, bf16[256,256]{1,0:T(8,128)(2,1)S(1)}, u32[]{:S(2)}, u32[]{:S(2)}) collective-permute-start(bf16[256,256]{1,0:T(8,128)(2,1)S(1)} %get-tuple-element.60), channel_id=1, source_target_pairs={{0,8},{8,16},{16,24},{24,28},{28,20},{20,12},{12,4},{4,0},{1,9},{9... | collective-permute-start | bytes 393224 | tf_op jit(solution)/shard_map/ppermute | solution.py:62
  41.5 7.3 %collective-permute-start.21 = (bf16[256,256]{1,0:T(8,128)(2,1)S(1)}, bf16[256,256]{1,0:T(8,128)(2,1)S(1)}, u32[]{:S(2)}, u32[]{:S(2)}) collective-permute-start(bf16[256,256]{1,0:T(8,128)(2,1)S(1)} %get-tuple-element.50.refs_0_), channel_id=1, source_target_pairs={{0,2},{1,3},{2,0},{3,1},{4,6},{5,7},{6,4},{7,5},{8,10},{9,11},{10,... | collective-permute-start | bytes 393224 | tf_op jit(solution)/shard_map/ppermute | solution.py:76
  42.3 11.6 %collective-permute-start.20 = (bf16[256,256]{1,0:T(8,128)(2,1)S(1)}, bf16[256,256]{1,0:T(8,128)(2,1)S(1)}, u32[]{:S(2)}, u32[]{:S(2)}) collective-permute-start(bf16[256,256]{1,0:T(8,128)(2,1)S(1)} %get-tuple-element.50.refs_0_), channel_id=1, source_target_pairs={{0,1},{1,0},{2,3},{3,2},{4,5},{5,4},{6,7},{7,6},{8,9},{9,8},{10,11... | collective-permute-start | bytes 393224 | tf_op jit(solution)/shard_map/ppermute | solution.py:76
  42.3 5.9 %collective-permute-start.34 = (bf16[256,256]{1,0:T(8,128)(2,1)S(1)}, bf16[256,256]{1,0:T(8,128)(2,1)S(1)}, u32[]{:S(2)}, u32[]{:S(2)}) collective-permute-start(bf16[256,256]{1,0:T(8,128)(2,1)S(1)} %get-tuple-element.64), channel_id=1, source_target_pairs={{0,4},{8,0},{16,8},{24,16},{28,24},{20,28},{12,20},{4,12},{1,5},{9... | collective-permute-start | bytes 393224 | tf_op jit(solution)/shard_map/ppermute | solution.py:62
  44.9 5.0 %collective-permute-start.31 = (bf16[256,256]{1,0:T(8,128)(2,1)S(1)}, bf16[256,256]{1,0:T(8,128)(2,1)S(1)}, u32[]{:S(2)}, u32[]{:S(2)}) collective-permute-start(bf16[256,256]{1,0:T(8,128)(2,1)S(1)} %add_convert_fusion.5), channel_id=1, source_target_pairs={{0,8},{8,16},{16,24},{24,28},{28,20},{20,12},{12,4},{4,0},{1,9},{9... | collective-permute-start | bytes 393224 | tf_op jit(solution)/shard_map/ppermute | solution.py:62
  48.2 5.1 %collective-permute-start.35 = (bf16[256,256]{1,0:T(8,128)(2,1)S(1)}, bf16[256,256]{1,0:T(8,128)(2,1)S(1)}, u32[]{:S(2)}, u32[]{:S(2)}) collective-permute-start(bf16[256,256]{1,0:T(8,128)(2,1)S(1)} %add_convert_fusion.2), channel_id=1, source_target_pairs={{0,4},{8,0},{16,8},{24,16},{28,24},{20,28},{12,20},{4,12},{1,5},{9... | collective-permute-start | bytes 393224 | tf_op jit(solution)/shard_map/ppermute | solution.py:62
  48.7 5.1 %collective-permute-start.22 = (bf16[256,256]{1,0:T(8,128)(2,1)S(1)}, bf16[256,256]{1,0:T(8,128)(2,1)S(1)}, u32[]{:S(2)}, u32[]{:S(2)}) collective-permute-start(bf16[256,256]{1,0:T(8,128)(2,1)S(1)} %collective-permute-done.21.refs_2_), channel_id=1, source_target_pairs={{0,1},{1,0},{2,3},{3,2},{4,5},{5,4},{6,7},{7,6},{8,9},{9,8},{10,11... | collective-permute-start | bytes 393224 | tf_op jit(solution)/shard_map/ppermute | solution.py:76
  50.0 7.0 %collective-permute-start.32 = (bf16[256,256]{1,0:T(8,128)(2,1)S(1)}, bf16[256,256]{1,0:T(8,128)(2,1)S(1)}, u32[]{:S(2)}, u32[]{:S(2)}) collective-permute-start(bf16[256,256]{1,0:T(8,128)(2,1)S(1)} %add_convert_fusion.4), channel_id=1, source_target_pairs={{0,8},{8,16},{16,24},{24,28},{28,20},{20,12},{12,4},{4,0},{1,9},{9... | collective-permute-start | bytes 393224 | tf_op jit(solution)/shard_map/ppermute | solution.py:62
  53.4 9.4 %collective-permute-start.36 = (bf16[256,256]{1,0:T(8,128)(2,1)S(1)}, bf16[256,256]{1,0:T(8,128)(2,1)S(1)}, u32[]{:S(2)}, u32[]{:S(2)}) collective-permute-start(bf16[256,256]{1,0:T(8,128)(2,1)S(1)} %add_convert_fusion.1), channel_id=1, source_target_pairs={{0,4},{8,0},{16,8},{24,16},{28,24},{20,28},{12,20},{4,12},{1,5},{9... | collective-permute-start | bytes 393224 | tf_op jit(solution)/shard_map/ppermute | solution.py:65
  54.8 5.7 %collective-permute-start.23 = (bf16[256,256]{1,0:T(8,128)(2,1)S(1)}, bf16[256,256]{1,0:T(8,128)(2,1)S(1)}, u32[]{:S(2)}, u32[]{:S(2)}) collective-permute-start(bf16[256,256]{1,0:T(8,128)(2,1)S(1)} %get-tuple-element.52), channel_id=1, source_target_pairs={{0,8},{8,16},{16,24},{24,28},{28,20},{20,12},{12,4},{4,0},{1,9},{9... | collective-permute-start | bytes 393224 | tf_op jit(solution)/shard_map/ppermute | solution.py:62
  56.5 5.7 %collective-permute-start.26 = (bf16[256,256]{1,0:T(8,128)(2,1)S(1)}, bf16[256,256]{1,0:T(8,128)(2,1)S(1)}, u32[]{:S(2)}, u32[]{:S(2)}) collective-permute-start(bf16[256,256]{1,0:T(8,128)(2,1)S(1)} %get-tuple-element.55), channel_id=1, source_target_pairs={{0,4},{8,0},{16,8},{24,16},{28,24},{20,28},{12,20},{4,12},{1,5},{9... | collective-permute-start | bytes 393224 | tf_op jit(solution)/shard_map/ppermute | solution.py:62
  57.0 6.2 %collective-permute-start.33 = (bf16[256,256]{1,0:T(8,128)(2,1)S(1)}, bf16[256,256]{1,0:T(8,128)(2,1)S(1)}, u32[]{:S(2)}, u32[]{:S(2)}) collective-permute-start(bf16[256,256]{1,0:T(8,128)(2,1)S(1)} %add_convert_fusion.3), channel_id=1, source_target_pairs={{0,8},{8,16},{16,24},{24,28},{28,20},{20,12},{12,4},{4,0},{1,9},{9... | collective-permute-start | bytes 393224 | tf_op jit(solution)/shard_map/ppermute | solution.py:65
  60.6 7.2 %collective-permute-start.24 = (bf16[256,256]{1,0:T(8,128)(2,1)S(1)}, bf16[256,256]{1,0:T(8,128)(2,1)S(1)}, u32[]{:S(2)}, u32[]{:S(2)}) collective-permute-start(bf16[256,256]{1,0:T(8,128)(2,1)S(1)} %add_convert_fusion.11), channel_id=1, source_target_pairs={{0,8},{8,16},{16,24},{24,28},{28,20},{20,12},{12,4},{4,0},{1,9},{9... | collective-permute-start | bytes 393224 | tf_op jit(solution)/shard_map/ppermute | solution.py:62
  62.2 5.0 %collective-permute-start.27 = (bf16[256,256]{1,0:T(8,128)(2,1)S(1)}, bf16[256,256]{1,0:T(8,128)(2,1)S(1)}, u32[]{:S(2)}, u32[]{:S(2)}) collective-permute-start(bf16[256,256]{1,0:T(8,128)(2,1)S(1)} %add_convert_fusion.9), channel_id=1, source_target_pairs={{0,4},{8,0},{16,8},{24,16},{28,24},{20,28},{12,20},{4,12},{1,5},{9... | collective-permute-start | bytes 393224 | tf_op jit(solution)/shard_map/ppermute | solution.py:62
  63.2 6.2 %collective-permute-start.38 = (bf16[256,256]{1,0:T(8,128)(2,1)S(1)}, bf16[256,256]{1,0:T(8,128)(2,1)S(1)}, u32[]{:S(2)}, u32[]{:S(2)}) collective-permute-start(bf16[256,256]{1,0:T(8,128)(2,1)S(1)} %add_convert_fusion.refs_0_), channel_id=1, source_target_pairs={{0,2},{1,3},{2,0},{3,1},{4,6},{5,7},{6,4},{7,5},{8,10},{9,11},{10,... | collective-permute-start | bytes 393224 | tf_op jit(solution)/shard_map/ppermute | solution.py:76
  64.5 8.4 %collective-permute-start.37 = (bf16[256,256]{1,0:T(8,128)(2,1)S(1)}, bf16[256,256]{1,0:T(8,128)(2,1)S(1)}, u32[]{:S(2)}, u32[]{:S(2)}) collective-permute-start(bf16[256,256]{1,0:T(8,128)(2,1)S(1)} %add_convert_fusion.refs_0_), channel_id=1, source_target_pairs={{0,1},{1,0},{2,3},{3,2},{4,5},{5,4},{6,7},{7,6},{8,9},{9,8},{10,11... | collective-permute-start | bytes 393224 | tf_op jit(solution)/shard_map/ppermute | solution.py:76
  67.8 6.0 %collective-permute-start.25 = (bf16[256,256]{1,0:T(8,128)(2,1)S(1)}, bf16[256,256]{1,0:T(8,128)(2,1)S(1)}, u32[]{:S(2)}, u32[]{:S(2)}) collective-permute-start(bf16[256,256]{1,0:T(8,128)(2,1)S(1)} %add_convert_fusion.10), channel_id=1, source_target_pairs={{0,8},{8,16},{16,24},{24,28},{28,20},{20,12},{12,4},{4,0},{1,9},{9... | collective-permute-start | bytes 393224 | tf_op jit(solution)/shard_map/ppermute | solution.py:65
  (16 other events, 135.3 us)
where the time goes:
time: 78.2 us; the launch traced here: 78.1 us
  starting transfers between devices  36.3 us (46%)
  waiting for transfers between devices  30.1 us (38%)
  Pallas kernels  9.02 us (12%)
  between operations  1.5 us (2%)
  other arithmetic  1.15 us (1%)
    ppermute x14, waiting for transfers between devices, ring_scatter(): held = lax.ppermute(held, 'paper', ring_pairs(count, step))  18.2 us
    ppermute x14, starting transfers between devices, ring_gather(): held = lax.ppermute(held, 'paper', ring_pairs(count, step))  15.8 us
    ppermute x14, starting transfers between devices, ring_scatter(): held = lax.ppermute(held, 'paper', ring_pairs(count, step))  14.8 us
    ppermute x14, waiting for transfers between devices, ring_gather(): held = lax.ppermute(held, 'paper', ring_pairs(count, step))  10.4 us
    ppermute x12, starting transfers between devices, feature_gather(): parts[r ^ bit] = lax.ppermute(held, 'author', pairs)  5.65 us
    pallas_call x6, Pallas kernels, run(): pl.pallas_call(kernel, in_specs=[SMEM] + [VMEM] * (len(inputs) + len(afte...  4.53 us
    pallas_call x2, Pallas kernels, adjacency(): call(mine, *tables, placed(tiles, near), *[placed(v, near) for v in after])  2.4 us
    pallas_call x1, Pallas kernels, fetch(): *found, scalars = call(places, live, *sources)  2.08 us
  transfers between devices with their start and end apart: 40, of which 16 were waited for; matrix products, arithmetic and copies ran while one was open for 1% of the time, Pallas kernels for 10%

commit v1 on v0

--- a/solution.py
+++ b/solution.py
@@ -53,7 +53,7 @@
 
 def ring_scatter(partials, count, first):
     ups = count // 2 if first > 0 else (count - 1) // 2
-    total = partials[0]
+    terms = [partials[0]]
     for reach, step in ((ups, 1), (count - 1 - ups, -1)):
         if reach == 0:
             continue
@@ -63,8 +63,8 @@
             held = held.astype(jnp.float32) + partials[place * step % count].astype(jnp.float32)
             held = held.astype(jnp.bfloat16)
         held = lax.ppermute(held, "paper", ring_pairs(count, step))
-        total = total + held.astype(jnp.float32)
-    return total
+        terms.append(held)
+    return terms
 
 
 def feature_gather(part, count):
@@ -102,7 +102,7 @@
         acc_ref[place] += (live / edges) * tiles_ref[tile].astype(jnp.float32)
         return carry
 
-    lax.fori_loop(0, tiles_ref.shape[0], add, 0, unroll=2)
+    lax.fori_loop(0, tiles_ref.shape[0], add, 0, unroll=8)
 
     def store(group, carry):
         for i in range(down):
@@ -238,8 +238,7 @@
 
 def layer_kernel(peers, mine_ref, *refs):
     blocks = refs[:peers]
-    adj_ref, kept_ref, feat_ref, cot_ref, write_adj_ref, out_ref, grad_ref = refs[peers:peers + 7]
-    partial_refs = refs[peers + 7:]
+    adj_ref, kept_ref, feat_ref, cot_ref, out_ref, grad_ref = refs[peers:]
     preact = kept_ref[...]
     for i in range(peers):
         preact = preact + matmul(adj_ref[i], blocks[i][...])
@@ -248,8 +247,12 @@
     slope = sigma * (1.0 + preact * (1.0 - sigma))
     grad = (cot_ref[...].astype(jnp.float32) * slope).astype(jnp.bfloat16)
     grad_ref[...] = grad
-    for i in range(peers):
-        partial_refs[i][...] = matmul_rows(write_adj_ref[i], grad).astype(partial_refs[i].dtype)
+
+
+def share_kernel(peers, mine_ref, grad_ref, adj_ref, *partial_refs):
+    grad = grad_ref[...]
+    for i in range(peers - 1, -1, -1):
+        partial_refs[i][...] = matmul_rows(adj_ref[i], grad).astype(partial_refs[i].dtype)
 
 
 def back_kernel(columns, mine_ref, *refs):
@@ -267,8 +270,14 @@
 
 
 def leave_kernel(columns, mine_ref, *refs):
-    parts, (weight_ref, out_ref) = refs[:columns], refs[columns:]
-    out_ref[...] = project_back_sum(mine_ref[1], parts, weight_ref).astype(jnp.bfloat16)
+    parts, (weight_ref, kept_ref, *terms) = refs[:columns], refs[columns:-3]
+    out_ref, paper_ref, author_ref = refs[-3:]
+    out_ref[...] = kept_ref[...]
+    total = terms[0][...]
+    for term in terms[1:]:
+        total = total + term[...].astype(jnp.float32)
+    paper_ref[...] = total.astype(jnp.bfloat16)
+    author_ref[...] = project_back_sum(mine_ref[1], parts, weight_ref).astype(jnp.bfloat16)
 
 
 def body(
@@ -335,24 +344,28 @@
         functools.partial(more_kernel, columns), mine, [*writes, write_window, kept],
         [(paper_tile, f32)], near,
     )
-    paper_out, grad_pre, *author_partials = run(
+    paper_out, grad_pre = run(
         functools.partial(layer_kernel, peers), mine,
-        [*sources, cite_adj, kept, paper_feat, cotangent, write_adj],
-        [(paper_tile, bf16), (paper_tile, bf16), (author_tile, f32)]
-        + [(author_tile, bf16)] * (peers - 1), near, kept=(0,),
+        [*sources, cite_adj, kept, paper_feat, cotangent], [(paper_tile, bf16), (paper_tile, bf16)], near,
+    )
+    author_partials = run(
+        functools.partial(share_kernel, peers), mine, [grad_pre, write_adj],
+        [(author_tile, f32)] + [(author_tile, bf16)] * (peers - 1), near,
     )
     grads = feature_gather(grad_pre, columns)
-    author_sum = ring_scatter(author_partials, peers, 1).astype(bf16)
+    author_terms = ring_scatter(author_partials, peers, 1)
+    author_sum = sum(term.astype(f32) for term in author_terms).astype(bf16)
     paper_partials = run(
         functools.partial(back_kernel, columns), mine,
         [*grads, w_cite, w_self, cite_adj, cotangent],
         [(paper_tile, f32)] + [(paper_tile, bf16)] * (peers - 1), near,
     )
-    paper_grad = ring_scatter(paper_partials, peers, -1).astype(bf16)
+    paper_terms = ring_scatter(paper_partials, peers, -1)
     author_sums = feature_gather(author_sum, columns)
-    author_grad, = run(
-        functools.partial(leave_kernel, columns), mine, [*author_sums, w_write],
-        [(author_tile, bf16)], near, kept=(0,),
+    paper_out, paper_grad, author_grad = run(
+        functools.partial(leave_kernel, columns), mine,
+        [*author_sums, w_write, paper_out, *paper_terms],
+        [(paper_tile, bf16), (paper_tile, bf16), (author_tile, bf16)], near, kept=(0, 1, 2),
     )
     return (paper_out, paper_grad, author_grad)
 

time: 78.2 us -> 76.3 us (0.976)
    pallas_call x6 -> x7, Pallas kernels: 4.53 us -> 4.15 us  [run(): pl.pallas_call(kernel, in_specs=[SMEM] + [VMEM] * (len(inputs) + len(afte...]
  transfers between devices with their start and end apart: 40 -> 40, of which waited for: 16 -> 14; matrix products, arithmetic and copies ran while one was open for 1% -> 1% of each run, Pallas kernels for 10% -> 8%
where the time goes in v1:
time: 76.3 us; the launch traced here: 76.2 us
  starting transfers between devices  36.2 us (47%)
  waiting for transfers between devices  29.8 us (39%)
  Pallas kernels  8.26 us (11%)
  between operations  1.52 us (2%)
    ppermute x14, waiting for transfers between devices, ring_scatter(): held = lax.ppermute(held, 'paper', ring_pairs(count, step))  17.5 us
    ppermute x14, starting transfers between devices, ring_gather(): held = lax.ppermute(held, 'paper', ring_pairs(count, step))  15.8 us
    ppermute x14, starting transfers between devices, ring_scatter(): held = lax.ppermute(held, 'paper', ring_pairs(count, step))  14.7 us
    ppermute x14, waiting for transfers between devices, ring_gather(): held = lax.ppermute(held, 'paper', ring_pairs(count, step))  10.8 us
    ppermute x12, starting transfers between devices, feature_gather(): parts[r ^ bit] = lax.ppermute(held, 'author', pairs)  5.66 us
    pallas_call x7, Pallas kernels, run(): pl.pallas_call(kernel, in_specs=[SMEM] + [VMEM] * (len(inputs) + len(afte...  4.15 us
    pallas_call x1, Pallas kernels, fetch(): *found, scalars = call(places, live, *sources)  2.08 us
    pallas_call x2, Pallas kernels, adjacency(): call(mine, *tables, placed(tiles, near), *[placed(v, near) for v in after])  2.02 us
  transfers between devices with their start and end apart: 40, of which 14 were waited for; matrix products, arithmetic and copies ran while one was open for 1% of the time, Pallas kernels for 8%

profile of v1, /device:TPU:0, one launch (start us, length us, event | category | flops | bytes accessed | tf_op | source)
XLA Modules:
  0.0 76.2 jit_solution(10686878741195731265)
XLA Ops:
  0.6 3.1 %collective-permute-start.13 = (bf16[256,256]{1,0:T(8,128)(2,1)}, bf16[256,256]{1,0:T(8,128)(2,1)S(1)}, u32[]{:S(2)}, u32[]{:S(2)}) collective-permute-start(bf16[256,256]{1,0:T(8,128)(2,1)} %refs_0_.5), channel_id=1, source_target_pairs={{0,8},{8,16},{16,24},{24,28},{28,20},{20,12},{12,4},{4,0},{1,9},{9... | collective-permute-start | bytes 393224 | tf_op jit(solution)/shard_map/ppermute | solution.py:49
  3.7 1.5 %collective-permute-start.1 = (bf16[256,256]{1,0:T(8,128)(2,1)}, bf16[256,256]{1,0:T(8,128)(2,1)S(1)}, u32[]{:S(2)}, u32[]{:S(2)}) collective-permute-start(bf16[256,256]{1,0:T(8,128)(2,1)} %refs_10_.3), channel_id=1, source_target_pairs={{0,2},{1,3},{2,0},{3,1},{4,6},{5,7},{6,4},{7,5},{8,10},{9,11},{10,... | collective-permute-start | bytes 393224 | tf_op jit(solution)/shard_map/ppermute | solution.py:76
  5.7 1.7 %collective-permute-done.13.refs_7_ = bf16[256,256]{1,0:T(8,128)(2,1)S(1)} collective-permute-done((bf16[256,256]{1,0:T(8,128)(2,1)}, bf16[256,256]{1,0:T(8,128)(2,1)S(1)}, u32[]{:S(2)}, u32[]{:S(2)}) %collective-permute-start.13) | collective-permute-done | bytes 131104 | tf_op jit(solution)/shard_map/ppermute | solution.py:49
  7.4 1.8 %collective-permute-start.14 = (bf16[256,256]{1,0:T(8,128)(2,1)S(1)}, bf16[256,256]{1,0:T(8,128)(2,1)S(1)}, u32[]{:S(2)}, u32[]{:S(2)}) collective-permute-start(bf16[256,256]{1,0:T(8,128)(2,1)S(1)} %collective-permute-done.13.refs_7_), channel_id=1, source_target_pairs={{0,8},{8,16},{16,24},{24,28},{28,20},{20,12},{12,4},{4,0},{1,9},{9... | collective-permute-start | bytes 393224 | tf_op jit(solution)/shard_map/ppermute | solution.py:49
  10.4 2.1 %shard_map.184 = (bf16[1024,256]{1,0:T(8,128)(2,1)S(1)}, bf16[1024,256]{1,0:T(8,128)(2,1)S(1)}, bf16[1024,256]{1,0:T(8,128)(2,1)S(1)}, s32[32]{0:T(128)S(4)}, s3...) custom-call(s32[2]{0:T(128)S(1)} %pad_add_fusion.place_ref, ...), custom_call_target="tpu_custom_call" | custom-call | tf_op jit(solution)/shard_map/pallas_call | solution.py:214
  12.8 1.8 %collective-permute-start.15 = (bf16[256,256]{1,0:T(8,128)(2,1)S(1)}, bf16[256,256]{1,0:T(8,128)(2,1)S(1)}, u32[]{:S(2)}, u32[]{:S(2)}) collective-permute-start(bf16[256,256]{1,0:T(8,128)(2,1)S(1)} %collective-permute-done.14.refs_6_), channel_id=1, source_target_pairs={{0,8},{8,16},{16,24},{24,28},{28,20},{20,12},{12,4},{4,0},{1,9},{9... | collective-permute-start | bytes 393224 | tf_op jit(solution)/shard_map/ppermute | solution.py:49
  15.4 3.5 %collective-permute-done.11.refs_2_ = bf16[256,256]{1,0:T(8,128)(2,1)S(1)} collective-permute-done((bf16[256,256]{1,0:T(8,128)(2,1)S(1)}, bf16[256,256]{1,0:T(8,128)(2,1)S(1)}, u32[]{:S(2)}, u32[]{:S(2)}) %collective-permute-start.11) | collective-permute-done | bytes 131104 | tf_op jit(solution)/shard_map/ppermute | solution.py:49
  19.1 1.8 %collective-permute-start.16 = (bf16[256,256]{1,0:T(8,128)(2,1)S(1)}, bf16[256,256]{1,0:T(8,128)(2,1)S(1)}, u32[]{:S(2)}, u32[]{:S(2)}) collective-permute-start(bf16[256,256]{1,0:T(8,128)(2,1)S(1)} %collective-permute-done.15.refs_5_), channel_id=1, source_target_pairs={{0,8},{8,16},{16,24},{24,28},{28,20},{20,12},{12,4},{4,0},{1,9},{9... | collective-permute-start | bytes 393224 | tf_op jit(solution)/shard_map/ppermute | solution.py:49
  20.9 1.6 %collective-permute-start.7 = (bf16[256,256]{1,0:T(8,128)(2,1)S(1)}, bf16[256,256]{1,0:T(8,128)(2,1)S(1)}, u32[]{:S(2)}, u32[]{:S(2)}) collective-permute-start(bf16[256,256]{1,0:T(8,128)(2,1)S(1)} %get-tuple-element.38.refs_0_), channel_id=1, source_target_pairs={{0,8},{8,16},{16,24},{24,28},{28,20},{20,12},{12,4},{4,0},{1,9},{9... | collective-permute-start | bytes 393224 | tf_op jit(solution)/shard_map/ppermute | solution.py:49
  25.3 1.6 %collective-permute-start.18 = (bf16[256,256]{1,0:T(8,128)(2,1)S(1)}, bf16[256,256]{1,0:T(8,128)(2,1)S(1)}, u32[]{:S(2)}, u32[]{:S(2)}) collective-permute-start(bf16[256,256]{1,0:T(8,128)(2,1)S(1)} %shard_map.188.refs_0_), channel_id=1, source_target_pairs={{0,2},{1,3},{2,0},{3,1},{4,6},{5,7},{6,4},{7,5},{8,10},{9,11},{10,... | collective-permute-start | bytes 393224 | tf_op jit(solution)/shard_map/ppermute | solution.py:76
  26.9 1.6 %collective-permute-start.8 = (bf16[256,256]{1,0:T(8,128)(2,1)S(1)}, bf16[256,256]{1,0:T(8,128)(2,1)S(1)}, u32[]{:S(2)}, u32[]{:S(2)}) collective-permute-start(bf16[256,256]{1,0:T(8,128)(2,1)S(1)} %collective-permute-done.7.refs_7_), channel_id=1, source_target_pairs={{0,8},{8,16},{16,24},{24,28},{28,20},{20,12},{12,4},{4,0},{1,9},{9... | collective-permute-start | bytes 393224 | tf_op jit(solution)/shard_map/ppermute | solution.py:49
  28.9 1.4 %collective-permute-done.18.refs_2_ = bf16[256,256]{1,0:T(8,128)(2,1)S(1)} collective-permute-done((bf16[256,256]{1,0:T(8,128)(2,1)S(1)}, bf16[256,256]{1,0:T(8,128)(2,1)S(1)}, u32[]{:S(2)}, u32[]{:S(2)}) %collective-permute-start.18) | collective-permute-done | bytes 131104 | tf_op jit(solution)/shard_map/ppermute | solution.py:76
  30.4 1.5 %collective-permute-done.8.refs_6_ = bf16[256,256]{1,0:T(8,128)(2,1)S(1)} collective-permute-done((bf16[256,256]{1,0:T(8,128)(2,1)S(1)}, bf16[256,256]{1,0:T(8,128)(2,1)S(1)}, u32[]{:S(2)}, u32[]{:S(2)}) %collective-permute-start.8) | collective-permute-done | bytes 131104 | tf_op jit(solution)/shard_map/ppermute | solution.py:49
  31.9 1.6 %collective-permute-start.9 = (bf16[256,256]{1,0:T(8,128)(2,1)S(1)}, bf16[256,256]{1,0:T(8,128)(2,1)S(1)}, u32[]{:S(2)}, u32[]{:S(2)}) collective-permute-start(bf16[256,256]{1,0:T(8,128)(2,1)S(1)} %collective-permute-done.8.refs_6_), channel_id=1, source_target_pairs={{0,8},{8,16},{16,24},{24,28},{28,20},{20,12},{12,4},{4,0},{1,9},{9... | collective-permute-start | bytes 393224 | tf_op jit(solution)/shard_map/ppermute | solution.py:49
  33.9 1.2 %shard_map.186.refs_8_.refs_6_ = bf16[8,256,256]{2,1,0:T(8,128)(2,1)S(1)} custom-call(s32[3]{0:T(128)S(4)} %get-tuple-element.35.mine_ref, s32[48]{0:T(128)S(4)} %get-tuple-element.39.owner_ref, s32[48]{0:T(128)S(4)} %get-tuple-element.40.inner_ref, s32[48]{0:T(128)S(4)} %get-tuple-element.41.outer_ref, s32[48]{0:T(128)S(4)} %get-tuple-element.42.edges_ref, ...), custom_call_target="tpu_custom_call" | custom-call | tf_op jit(solution)/shard_map/pallas_call | solution.py:130
  35.4 1.4 %collective-permute-done.9.refs_5_ = bf16[256,256]{1,0:T(8,128)(2,1)S(1)} collective-permute-done((bf16[256,256]{1,0:T(8,128)(2,1)S(1)}, bf16[256,256]{1,0:T(8,128)(2,1)S(1)}, u32[]{:S(2)}, u32[]{:S(2)}) %collective-permute-start.9) | collective-permute-done | bytes 131104 | tf_op jit(solution)/shard_map/ppermute | solution.py:49
  36.8 1.6 %collective-permute-done.6.refs_4_ = bf16[256,256]{1,0:T(8,128)(2,1)S(1)} collective-permute-done((bf16[256,256]{1,0:T(8,128)(2,1)S(1)}, bf16[256,256]{1,0:T(8,128)(2,1)S(1)}, u32[]{:S(2)}, u32[]{:S(2)}) %collective-permute-start.6) | collective-permute-done | bytes 131104 | tf_op jit(solution)/shard_map/ppermute | solution.py:49
  39.4 1.6 %collective-permute-start.20 = (bf16[256,256]{1,0:T(8,128)(2,1)S(1)}, bf16[256,256]{1,0:T(8,128)(2,1)S(1)}, u32[]{:S(2)}, u32[]{:S(2)}) collective-permute-start(bf16[256,256]{1,0:T(8,128)(2,1)S(1)} %get-tuple-element.51), channel_id=1, source_target_pairs={{0,8},{8,16},{16,24},{24,28},{28,20},{20,12},{12,4},{4,0},{1,9},{9... | collective-permute-start | bytes 393224 | tf_op jit(solution)/shard_map/ppermute | solution.py:62
  42.3 2.1 %collective-permute-done.20 = bf16[256,256]{1,0:T(8,128)(2,1)S(1)} collective-permute-done((bf16[256,256]{1,0:T(8,128)(2,1)S(1)}, bf16[256,256]{1,0:T(8,128)(2,1)S(1)}, u32[]{:S(2)}, u32[]{:S(2)}) %collective-permute-start.20) | collective-permute-done | bytes 131104 | tf_op jit(solution)/shard_map/ppermute | solution.py:62
  44.5 1.6 %collective-permute-start.21 = (bf16[256,256]{1,0:T(8,128)(2,1)S(1)}, bf16[256,256]{1,0:T(8,128)(2,1)S(1)}, u32[]{:S(2)}, u32[]{:S(2)}) collective-permute-start(bf16[256,256]{1,0:T(8,128)(2,1)S(1)} %add_convert_fusion.10), channel_id=1, source_target_pairs={{0,8},{8,16},{16,24},{24,28},{28,20},{20,12},{12,4},{4,0},{1,9},{9... | collective-permute-start | bytes 393224 | tf_op jit(solution)/shard_map/ppermute | solution.py:62
  46.1 1.7 %collective-permute-done.24 = bf16[256,256]{1,0:T(8,128)(2,1)S(1)} collective-permute-done((bf16[256,256]{1,0:T(8,128)(2,1)S(1)}, bf16[256,256]{1,0:T(8,128)(2,1)S(1)}, u32[]{:S(2)}, u32[]{:S(2)}) %collective-permute-start.24) | collective-permute-done | bytes 131104 | tf_op jit(solution)/shard_map/ppermute | solution.py:62
  49.8 1.6 %collective-permute-start.33 = (bf16[256,256]{1,0:T(8,128)(2,1)S(1)}, bf16[256,256]{1,0:T(8,128)(2,1)S(1)}, u32[]{:S(2)}, u32[]{:S(2)}) collective-permute-start(bf16[256,256]{1,0:T(8,128)(2,1)S(1)} %get-tuple-element.60), channel_id=1, source_target_pairs={{0,8},{8,16},{16,24},{24,28},{28,20},{20,12},{12,4},{4,0},{1,9},{9... | collective-permute-start | bytes 393224 | tf_op jit(solution)/shard_map/ppermute | solution.py:62
  51.4 1.6 %collective-permute-start.22 = (bf16[256,256]{1,0:T(8,128)(2,1)S(1)}, bf16[256,256]{1,0:T(8,128)(2,1)S(1)}, u32[]{:S(2)}, u32[]{:S(2)}) collective-permute-start(bf16[256,256]{1,0:T(8,128)(2,1)S(1)} %add_convert_fusion.9), channel_id=1, source_target_pairs={{0,8},{8,16},{16,24},{24,28},{28,20},{20,12},{12,4},{4,0},{1,9},{9... | collective-permute-start | bytes 393224 | tf_op jit(solution)/shard_map/ppermute | solution.py:62
  53.0 1.2 %collective-permute-done.25 = bf16[256,256]{1,0:T(8,128)(2,1)S(1)} collective-permute-done((bf16[256,256]{1,0:T(8,128)(2,1)S(1)}, bf16[256,256]{1,0:T(8,128)(2,1)S(1)}, u32[]{:S(2)}, u32[]{:S(2)}) %collective-permute-start.25) | collective-permute-done | bytes 131104 | tf_op jit(solution)/shard_map/ppermute | solution.py:62
  54.8 2.3 %collective-permute-done.36 = bf16[256,256]{1,0:T(8,128)(2,1)S(1)} collective-permute-done((bf16[256,256]{1,0:T(8,128)(2,1)S(1)}, bf16[256,256]{1,0:T(8,128)(2,1)S(1)}, u32[]{:S(2)}, u32[]{:S(2)}) %collective-permute-start.36) | collective-permute-done | bytes 131104 | tf_op jit(solution)/shard_map/ppermute | solution.py:62
  57.6 1.6 %collective-permute-start.23 = (bf16[256,256]{1,0:T(8,128)(2,1)S(1)}, bf16[256,256]{1,0:T(8,128)(2,1)S(1)}, u32[]{:S(2)}, u32[]{:S(2)}) collective-permute-start(bf16[256,256]{1,0:T(8,128)(2,1)S(1)} %add_convert_fusion.8), channel_id=1, source_target_pairs={{0,8},{8,16},{16,24},{24,28},{28,20},{20,12},{12,4},{4,0},{1,9},{9... | collective-permute-start | bytes 393224 | tf_op jit(solution)/shard_map/ppermute | solution.py:65
  59.3 1.5 %collective-permute-start.34 = (bf16[256,256]{1,0:T(8,128)(2,1)S(1)}, bf16[256,256]{1,0:T(8,128)(2,1)S(1)}, u32[]{:S(2)}, u32[]{:S(2)}) collective-permute-start(bf16[256,256]{1,0:T(8,128)(2,1)S(1)} %add_convert_fusion.4), channel_id=1, source_target_pairs={{0,8},{8,16},{16,24},{24,28},{28,20},{20,12},{12,4},{4,0},{1,9},{9... | collective-permute-start | bytes 393224 | tf_op jit(solution)/shard_map/ppermute | solution.py:62
  60.8 1.8 %collective-permute-done.23 = bf16[256,256]{1,0:T(8,128)(2,1)S(1)} collective-permute-done((bf16[256,256]{1,0:T(8,128)(2,1)S(1)}, bf16[256,256]{1,0:T(8,128)(2,1)S(1)}, u32[]{:S(2)}, u32[]{:S(2)}) %collective-permute-start.23) | collective-permute-done | bytes 131104 | tf_op jit(solution)/shard_map/ppermute | solution.py:65
  62.7 1.3 %collective-permute-start.28 = (bf16[256,256]{1,0:T(8,128)(2,1)S(1)}, bf16[256,256]{1,0:T(8,128)(2,1)S(1)}, u32[]{:S(2)}, u32[]{:S(2)}) collective-permute-start(bf16[256,256]{1,0:T(8,128)(2,1)S(1)} %add_convert_fusion.5.refs_0_), channel_id=1, source_target_pairs={{0,2},{1,3},{2,0},{3,1},{4,6},{5,7},{6,4},{7,5},{8,10},{9,11},{10,... | collective-permute-start | bytes 393224 | tf_op jit(solution)/shard_map/ppermute | solution.py:76
  64.5 1.7 %collective-permute-start.35 = (bf16[256,256]{1,0:T(8,128)(2,1)S(1)}, bf16[256,256]{1,0:T(8,128)(2,1)S(1)}, u32[]{:S(2)}, u32[]{:S(2)}) collective-permute-start(bf16[256,256]{1,0:T(8,128)(2,1)S(1)} %add_convert_fusion.3), channel_id=1, source_target_pairs={{0,8},{8,16},{16,24},{24,28},{28,20},{20,12},{12,4},{4,0},{1,9},{9... | collective-permute-start | bytes 393224 | tf_op jit(solution)/shard_map/ppermute | solution.py:65
  66.2 3.8 %collective-permute-done.38 = bf16[256,256]{1,0:T(8,128)(2,1)S(1)} collective-permute-done((bf16[256,256]{1,0:T(8,128)(2,1)S(1)}, bf16[256,256]{1,0:T(8,128)(2,1)S(1)}, u32[]{:S(2)}, u32[]{:S(2)}) %collective-permute-start.38) | collective-permute-done | bytes 131104 | tf_op jit(solution)/shard_map/ppermute | solution.py:62
  70.5 4.6 %collective-permute-done.39.refs_8_ = bf16[256,256]{1,0:T(8,128)(2,1)S(1)} collective-permute-done((bf16[256,256]{1,0:T(8,128)(2,1)S(1)}, bf16[256,256]{1,0:T(8,128)(2,1)S(1)}, u32[]{:S(2)}, u32[]{:S(2)}) %collective-permute-start.39) | collective-permute-done | bytes 131104 | tf_op jit(solution)/shard_map/ppermute | solution.py:65
  (86 shorter events, 14.0 us)
Async XLA Ops:
  0.6 6.8 %collective-permute-start.13 = (bf16[256,256]{1,0:T(8,128)(2,1)}, bf16[256,256]{1,0:T(8,128)(2,1)S(1)}, u32[]{:S(2)}, u32[]{:S(2)}) collective-permute-start(bf16[256,256]{1,0:T(8,128)(2,1)} %refs_0_.5), channel_id=1, source_target_pairs={{0,8},{8,16},{16,24},{24,28},{28,20},{20,12},{12,4},{4,0},{1,9},{9... | collective-permute-start | bytes 393224 | tf_op jit(solution)/shard_map/ppermute | solution.py:49
  3.7 5.5 %collective-permute-start.1 = (bf16[256,256]{1,0:T(8,128)(2,1)}, bf16[256,256]{1,0:T(8,128)(2,1)S(1)}, u32[]{:S(2)}, u32[]{:S(2)}) collective-permute-start(bf16[256,256]{1,0:T(8,128)(2,1)} %refs_10_.3), channel_id=1, source_target_pairs={{0,2},{1,3},{2,0},{3,1},{4,6},{5,7},{6,4},{7,5},{8,10},{9,11},{10,... | collective-permute-start | bytes 393224 | tf_op jit(solution)/shard_map/ppermute | solution.py:76
  5.2 7.3 %collective-permute-start.10 = (bf16[256,256]{1,0:T(8,128)(2,1)}, bf16[256,256]{1,0:T(8,128)(2,1)S(1)}, u32[]{:S(2)}, u32[]{:S(2)}) collective-permute-start(bf16[256,256]{1,0:T(8,128)(2,1)} %refs_0_.5), channel_id=1, source_target_pairs={{0,4},{8,0},{16,8},{24,16},{28,24},{20,28},{12,20},{4,12},{1,5},{9... | collective-permute-start | bytes 393224 | tf_op jit(solution)/shard_map/ppermute | solution.py:49
  7.4 5.5 %collective-permute-start.14 = (bf16[256,256]{1,0:T(8,128)(2,1)S(1)}, bf16[256,256]{1,0:T(8,128)(2,1)S(1)}, u32[]{:S(2)}, u32[]{:S(2)}) collective-permute-start(bf16[256,256]{1,0:T(8,128)(2,1)S(1)} %collective-permute-done.13.refs_7_), channel_id=1, source_target_pairs={{0,8},{8,16},{16,24},{24,28},{28,20},{20,12},{12,4},{4,0},{1,9},{9... | collective-permute-start | bytes 393224 | tf_op jit(solution)/shard_map/ppermute | solution.py:49
  9.2 5.5 %collective-permute-start = (bf16[256,256]{1,0:T(8,128)(2,1)}, bf16[256,256]{1,0:T(8,128)(2,1)S(1)}, u32[]{:S(2)}, u32[]{:S(2)}) collective-permute-start(bf16[256,256]{1,0:T(8,128)(2,1)} %refs_10_.3), channel_id=1, source_target_pairs={{0,1},{1,0},{2,3},{3,2},{4,5},{5,4},{6,7},{7,6},{8,9},{9,8},{10,11... | collective-permute-start | bytes 393224 | tf_op jit(solution)/shard_map/ppermute | solution.py:76
  9.2 5.5 %collective-permute-start.2 = (bf16[256,256]{1,0:T(8,128)(2,1)S(1)}, bf16[256,256]{1,0:T(8,128)(2,1)S(1)}, u32[]{:S(2)}, u32[]{:S(2)}) collective-permute-start(bf16[256,256]{1,0:T(8,128)(2,1)S(1)} %collective-permute-done.1.refs_2_), channel_id=1, source_target_pairs={{0,1},{1,0},{2,3},{3,2},{4,5},{5,4},{6,7},{7,6},{8,9},{9,8},{10,11... | collective-permute-start | bytes 393224 | tf_op jit(solution)/shard_map/ppermute | solution.py:76
  12.6 6.3 %collective-permute-start.11 = (bf16[256,256]{1,0:T(8,128)(2,1)S(1)}, bf16[256,256]{1,0:T(8,128)(2,1)S(1)}, u32[]{:S(2)}, u32[]{:S(2)}) collective-permute-start(bf16[256,256]{1,0:T(8,128)(2,1)S(1)} %collective-permute-done.10.refs_1_), channel_id=1, source_target_pairs={{0,4},{8,0},{16,8},{24,16},{28,24},{20,28},{12,20},{4,12},{1,5},{9... | collective-permute-start | bytes 393224 | tf_op jit(solution)/shard_map/ppermute | solution.py:49
  12.8 6.2 %collective-permute-start.15 = (bf16[256,256]{1,0:T(8,128)(2,1)S(1)}, bf16[256,256]{1,0:T(8,128)(2,1)S(1)}, u32[]{:S(2)}, u32[]{:S(2)}) collective-permute-start(bf16[256,256]{1,0:T(8,128)(2,1)S(1)} %collective-permute-done.14.refs_6_), channel_id=1, source_target_pairs={{0,8},{8,16},{16,24},{24,28},{28,20},{20,12},{12,4},{4,0},{1,9},{9... | collective-permute-start | bytes 393224 | tf_op jit(solution)/shard_map/ppermute | solution.py:49
  15.1 7.3 %collective-permute-start.3 = (bf16[256,256]{1,0:T(8,128)(2,1)S(1)}, bf16[256,256]{1,0:T(8,128)(2,1)S(1)}, u32[]{:S(2)}, u32[]{:S(2)}) collective-permute-start(bf16[256,256]{1,0:T(8,128)(2,1)S(1)} %get-tuple-element.38.refs_0_), channel_id=1, source_target_pairs={{0,4},{8,0},{16,8},{24,16},{28,24},{20,28},{12,20},{4,12},{1,5},{9... | collective-permute-start | bytes 393224 | tf_op jit(solution)/shard_map/ppermute | solution.py:49
  18.8 6.1 %collective-permute-start.12 = (bf16[256,256]{1,0:T(8,128)(2,1)S(1)}, bf16[256,256]{1,0:T(8,128)(2,1)S(1)}, u32[]{:S(2)}, u32[]{:S(2)}) collective-permute-start(bf16[256,256]{1,0:T(8,128)(2,1)S(1)} %collective-permute-done.11.refs_2_), channel_id=1, source_target_pairs={{0,4},{8,0},{16,8},{24,16},{28,24},{20,28},{12,20},{4,12},{1,5},{9... | collective-permute-start | bytes 393224 | tf_op jit(solution)/shard_map/ppermute | solution.py:49
  19.1 5.8 %collective-permute-start.16 = (bf16[256,256]{1,0:T(8,128)(2,1)S(1)}, bf16[256,256]{1,0:T(8,128)(2,1)S(1)}, u32[]{:S(2)}, u32[]{:S(2)}) collective-permute-start(bf16[256,256]{1,0:T(8,128)(2,1)S(1)} %collective-permute-done.15.refs_5_), channel_id=1, source_target_pairs={{0,8},{8,16},{16,24},{24,28},{28,20},{20,12},{12,4},{4,0},{1,9},{9... | collective-permute-start | bytes 393224 | tf_op jit(solution)/shard_map/ppermute | solution.py:49
  20.9 6.0 %collective-permute-start.7 = (bf16[256,256]{1,0:T(8,128)(2,1)S(1)}, bf16[256,256]{1,0:T(8,128)(2,1)S(1)}, u32[]{:S(2)}, u32[]{:S(2)}) collective-permute-start(bf16[256,256]{1,0:T(8,128)(2,1)S(1)} %get-tuple-element.38.refs_0_), channel_id=1, source_target_pairs={{0,8},{8,16},{16,24},{24,28},{28,20},{20,12},{12,4},{4,0},{1,9},{9... | collective-permute-start | bytes 393224 | tf_op jit(solution)/shard_map/ppermute | solution.py:49
  22.4 6.0 %collective-permute-start.4 = (bf16[256,256]{1,0:T(8,128)(2,1)S(1)}, bf16[256,256]{1,0:T(8,128)(2,1)S(1)}, u32[]{:S(2)}, u32[]{:S(2)}) collective-permute-start(bf16[256,256]{1,0:T(8,128)(2,1)S(1)} %collective-permute-done.3.refs_1_), channel_id=1, source_target_pairs={{0,4},{8,0},{16,8},{24,16},{28,24},{20,28},{12,20},{4,12},{1,5},{9... | collective-permute-start | bytes 393224 | tf_op jit(solution)/shard_map/ppermute | solution.py:49
  25.3 5.0 %collective-permute-start.18 = (bf16[256,256]{1,0:T(8,128)(2,1)S(1)}, bf16[256,256]{1,0:T(8,128)(2,1)S(1)}, u32[]{:S(2)}, u32[]{:S(2)}) collective-permute-start(bf16[256,256]{1,0:T(8,128)(2,1)S(1)} %shard_map.188.refs_0_), channel_id=1, source_target_pairs={{0,2},{1,3},{2,0},{3,1},{4,6},{5,7},{6,4},{7,5},{8,10},{9,11},{10,... | collective-permute-start | bytes 393224 | tf_op jit(solution)/shard_map/ppermute | solution.py:76
  28.9 6.1 %collective-permute-start.17 = (bf16[256,256]{1,0:T(8,128)(2,1)S(1)}, bf16[256,256]{1,0:T(8,128)(2,1)S(1)}, u32[]{:S(2)}, u32[]{:S(2)}) collective-permute-start(bf16[256,256]{1,0:T(8,128)(2,1)S(1)} %shard_map.188.refs_0_), channel_id=1, source_target_pairs={{0,1},{1,0},{2,3},{3,2},{4,5},{5,4},{6,7},{7,6},{8,9},{9,8},{10,11... | collective-permute-start | bytes 393224 | tf_op jit(solution)/shard_map/ppermute | solution.py:76
  39.4 5.0 %collective-permute-start.20 = (bf16[256,256]{1,0:T(8,128)(2,1)S(1)}, bf16[256,256]{1,0:T(8,128)(2,1)S(1)}, u32[]{:S(2)}, u32[]{:S(2)}) collective-permute-start(bf16[256,256]{1,0:T(8,128)(2,1)S(1)} %get-tuple-element.51), channel_id=1, source_target_pairs={{0,8},{8,16},{16,24},{24,28},{28,20},{20,12},{12,4},{4,0},{1,9},{9... | collective-permute-start | bytes 393224 | tf_op jit(solution)/shard_map/ppermute | solution.py:62
  41.0 5.1 %collective-permute-start.31 = (bf16[256,256]{1,0:T(8,128)(2,1)S(1)}, bf16[256,256]{1,0:T(8,128)(2,1)S(1)}, u32[]{:S(2)}, u32[]{:S(2)}) collective-permute-start(bf16[256,256]{1,0:T(8,128)(2,1)S(1)} %get-tuple-element.49.grad_ref.refs_0_), channel_id=1, source_target_pairs={{0,2},{1,3},{2,0},{3,1},{4,6},{5,7},{6,4},{7,5},{8,10},{9,11},{10,... | collective-permute-start | bytes 393224 | tf_op jit(solution)/shard_map/ppermute | solution.py:76
  41.8 6.5 %collective-permute-start.30 = (bf16[256,256]{1,0:T(8,128)(2,1)S(1)}, bf16[256,256]{1,0:T(8,128)(2,1)S(1)}, u32[]{:S(2)}, u32[]{:S(2)}) collective-permute-start(bf16[256,256]{1,0:T(8,128)(2,1)S(1)} %get-tuple-element.49.grad_ref.refs_0_), channel_id=1, source_target_pairs={{0,1},{1,0},{2,3},{3,2},{4,5},{5,4},{6,7},{7,6},{8,9},{9,8},{10,11... | collective-permute-start | bytes 393224 | tf_op jit(solution)/shard_map/ppermute | solution.py:76
  41.9 5.9 %collective-permute-start.24 = (bf16[256,256]{1,0:T(8,128)(2,1)S(1)}, bf16[256,256]{1,0:T(8,128)(2,1)S(1)}, u32[]{:S(2)}, u32[]{:S(2)}) collective-permute-start(bf16[256,256]{1,0:T(8,128)(2,1)S(1)} %get-tuple-element.55), channel_id=1, source_target_pairs={{0,4},{8,0},{16,8},{24,16},{28,24},{20,28},{12,20},{4,12},{1,5},{9... | collective-permute-start | bytes 393224 | tf_op jit(solution)/shard_map/ppermute | solution.py:62
  44.5 6.9 %collective-permute-start.21 = (bf16[256,256]{1,0:T(8,128)(2,1)S(1)}, bf16[256,256]{1,0:T(8,128)(2,1)S(1)}, u32[]{:S(2)}, u32[]{:S(2)}) collective-permute-start(bf16[256,256]{1,0:T(8,128)(2,1)S(1)} %add_convert_fusion.10), channel_id=1, source_target_pairs={{0,8},{8,16},{16,24},{24,28},{28,20},{20,12},{12,4},{4,0},{1,9},{9... | collective-permute-start | bytes 393224 | tf_op jit(solution)/shard_map/ppermute | solution.py:62
  47.8 6.4 %collective-permute-start.25 = (bf16[256,256]{1,0:T(8,128)(2,1)S(1)}, bf16[256,256]{1,0:T(8,128)(2,1)S(1)}, u32[]{:S(2)}, u32[]{:S(2)}) collective-permute-start(bf16[256,256]{1,0:T(8,128)(2,1)S(1)} %add_convert_fusion.7), channel_id=1, source_target_pairs={{0,4},{8,0},{16,8},{24,16},{28,24},{20,28},{12,20},{4,12},{1,5},{9... | collective-permute-start | bytes 393224 | tf_op jit(solution)/shard_map/ppermute | solution.py:62
  49.3 7.8 %collective-permute-start.36 = (bf16[256,256]{1,0:T(8,128)(2,1)S(1)}, bf16[256,256]{1,0:T(8,128)(2,1)S(1)}, u32[]{:S(2)}, u32[]{:S(2)}) collective-permute-start(bf16[256,256]{1,0:T(8,128)(2,1)S(1)} %get-tuple-element.63), channel_id=1, source_target_pairs={{0,4},{8,0},{16,8},{24,16},{28,24},{20,28},{12,20},{4,12},{1,5},{9... | collective-permute-start | bytes 393224 | tf_op jit(solution)/shard_map/ppermute | solution.py:62
  49.8 9.5 %collective-permute-start.33 = (bf16[256,256]{1,0:T(8,128)(2,1)S(1)}, bf16[256,256]{1,0:T(8,128)(2,1)S(1)}, u32[]{:S(2)}, u32[]{:S(2)}) collective-permute-start(bf16[256,256]{1,0:T(8,128)(2,1)S(1)} %get-tuple-element.60), channel_id=1, source_target_pairs={{0,8},{8,16},{16,24},{24,28},{28,20},{20,12},{12,4},{4,0},{1,9},{9... | collective-permute-start | bytes 393224 | tf_op jit(solution)/shard_map/ppermute | solution.py:62
  51.4 6.2 %collective-permute-start.22 = (bf16[256,256]{1,0:T(8,128)(2,1)S(1)}, bf16[256,256]{1,0:T(8,128)(2,1)S(1)}, u32[]{:S(2)}, u32[]{:S(2)}) collective-permute-start(bf16[256,256]{1,0:T(8,128)(2,1)S(1)} %add_convert_fusion.9), channel_id=1, source_target_pairs={{0,8},{8,16},{16,24},{24,28},{28,20},{20,12},{12,4},{4,0},{1,9},{9... | collective-permute-start | bytes 393224 | tf_op jit(solution)/shard_map/ppermute | solution.py:62
  54.3 6.5 %collective-permute-start.26 = (bf16[256,256]{1,0:T(8,128)(2,1)S(1)}, bf16[256,256]{1,0:T(8,128)(2,1)S(1)}, u32[]{:S(2)}, u32[]{:S(2)}) collective-permute-start(bf16[256,256]{1,0:T(8,128)(2,1)S(1)} %add_convert_fusion.6), channel_id=1, source_target_pairs={{0,4},{8,0},{16,8},{24,16},{28,24},{20,28},{12,20},{4,12},{1,5},{9... | collective-permute-start | bytes 393224 | tf_op jit(solution)/shard_map/ppermute | solution.py:65
  57.1 6.9 %collective-permute-start.37 = (bf16[256,256]{1,0:T(8,128)(2,1)S(1)}, bf16[256,256]{1,0:T(8,128)(2,1)S(1)}, u32[]{:S(2)}, u32[]{:S(2)}) collective-permute-start(bf16[256,256]{1,0:T(8,128)(2,1)S(1)} %add_convert_fusion.2), channel_id=1, source_target_pairs={{0,4},{8,0},{16,8},{24,16},{28,24},{20,28},{12,20},{4,12},{1,5},{9... | collective-permute-start | bytes 393224 | tf_op jit(solution)/shard_map/ppermute | solution.py:62
  59.3 5.2 %collective-permute-start.34 = (bf16[256,256]{1,0:T(8,128)(2,1)S(1)}, bf16[256,256]{1,0:T(8,128)(2,1)S(1)}, u32[]{:S(2)}, u32[]{:S(2)}) collective-permute-start(bf16[256,256]{1,0:T(8,128)(2,1)S(1)} %add_convert_fusion.4), channel_id=1, source_target_pairs={{0,8},{8,16},{16,24},{24,28},{28,20},{20,12},{12,4},{4,0},{1,9},{9... | collective-permute-start | bytes 393224 | tf_op jit(solution)/shard_map/ppermute | solution.py:62
  62.7 7.8 %collective-permute-start.28 = (bf16[256,256]{1,0:T(8,128)(2,1)S(1)}, bf16[256,256]{1,0:T(8,128)(2,1)S(1)}, u32[]{:S(2)}, u32[]{:S(2)}) collective-permute-start(bf16[256,256]{1,0:T(8,128)(2,1)S(1)} %add_convert_fusion.5.refs_0_), channel_id=1, source_target_pairs={{0,2},{1,3},{2,0},{3,1},{4,6},{5,7},{6,4},{7,5},{8,10},{9,11},{10,... | collective-permute-start | bytes 393224 | tf_op jit(solution)/shard_map/ppermute | solution.py:76
  64.0 6.5 %collective-permute-start.27 = (bf16[256,256]{1,0:T(8,128)(2,1)S(1)}, bf16[256,256]{1,0:T(8,128)(2,1)S(1)}, u32[]{:S(2)}, u32[]{:S(2)}) collective-permute-start(bf16[256,256]{1,0:T(8,128)(2,1)S(1)} %add_convert_fusion.5.refs_0_), channel_id=1, source_target_pairs={{0,1},{1,0},{2,3},{3,2},{4,5},{5,4},{6,7},{7,6},{8,9},{9,8},{10,11... | collective-permute-start | bytes 393224 | tf_op jit(solution)/shard_map/ppermute | solution.py:76
  64.0 6.0 %collective-permute-start.38 = (bf16[256,256]{1,0:T(8,128)(2,1)S(1)}, bf16[256,256]{1,0:T(8,128)(2,1)S(1)}, u32[]{:S(2)}, u32[]{:S(2)}) collective-permute-start(bf16[256,256]{1,0:T(8,128)(2,1)S(1)} %add_convert_fusion.1), channel_id=1, source_target_pairs={{0,4},{8,0},{16,8},{24,16},{28,24},{20,28},{12,20},{4,12},{1,5},{9... | collective-permute-start | bytes 393224 | tf_op jit(solution)/shard_map/ppermute | solution.py:62
  64.5 6.0 %collective-permute-start.35 = (bf16[256,256]{1,0:T(8,128)(2,1)S(1)}, bf16[256,256]{1,0:T(8,128)(2,1)S(1)}, u32[]{:S(2)}, u32[]{:S(2)}) collective-permute-start(bf16[256,256]{1,0:T(8,128)(2,1)S(1)} %add_convert_fusion.3), channel_id=1, source_target_pairs={{0,8},{8,16},{16,24},{24,28},{28,20},{20,12},{12,4},{4,0},{1,9},{9... | collective-permute-start | bytes 393224 | tf_op jit(solution)/shard_map/ppermute | solution.py:65
  70.0 5.1 %collective-permute-start.39 = (bf16[256,256]{1,0:T(8,128)(2,1)S(1)}, bf16[256,256]{1,0:T(8,128)(2,1)S(1)}, u32[]{:S(2)}, u32[]{:S(2)}) collective-permute-start(bf16[256,256]{1,0:T(8,128)(2,1)S(1)} %add_convert_fusion), channel_id=1, source_target_pairs={{0,4},{8,0},{16,8},{24,16},{28,24},{20,28},{12,20},{4,12},{1,5},{9... | collective-permute-start | bytes 393224 | tf_op jit(solution)/shard_map/ppermute | solution.py:65
  (16 other events, 130.6 us)
